TPU v7x, 32 devices: a whole 2x2x4 slice. The times are simulated.
32 devices in a mesh: row: 8 (over z, x), col: 4 (over y, core).
Axes of the slice: x: 2, y: 2, z: 4, core: 2. Of those that a mesh axis runs over, the one named last changes fastest.
Arguments:
- normal_matrix: float32 [4096, 4096], P('row', 'col'), as said below
Outputs:
- factored: float32 [4096, 4096], P('row', 'col')
- log_det: float32 [], replicated
Inputs may be any that keep to these rules, and one draw needn't show every extreme that they name: normal_matrix is symmetric and positive definite.
All inputs are finite; a program needn't handle non-finite values.
Results may differ from a plain program's by a relative error of at most 0.0001.
Values sent between devices are 32-bit elements; how exact they have to be, the bound alone decides.
No kernel may reach another device: no remote copies, remote signals or barrier semaphores. Data moves between devices by JAX's collectives and lax.ppermute only.
A program may use at most 64 MiB of HBM per device.

v0:
```python
import jax
import jax.numpy as jnp
from jax import lax
from jax.experimental import pallas as pl
from jax.experimental.pallas import tpu as pltpu
from jax.sharding import PartitionSpec as P

LANES = 128
SUB = 8
TILES = LANES // SUB
GROUP = 4


def block_index(k, j, count):
    return k * count - (k * (k - 1)) // 2 + (j - k)


def leaf(a_ref, w_ref, base):
    a = [a_ref[base + t] for t in range(TILES)]
    sub = lax.broadcasted_iota(jnp.int32, (SUB, LANES), 0)
    lane = lax.broadcasted_iota(jnp.int32, (SUB, LANES), 1)
    w = [jnp.where(lane == sub + SUB * t, 1.0, 0.0).astype(jnp.float32) for t in range(TILES)]
    logs = jnp.zeros((SUB, LANES), jnp.float32)
    shape = (SUB, LANES)
    for g in range(LANES // GROUP):
        i, q, first = (GROUP * g) // SUB, (GROUP * g) % SUB, GROUP * g
        rows = [jnp.broadcast_to(a[i][q + k : q + k + 1, :], shape) for k in range(GROUP)]
        wrows = [jnp.broadcast_to(w[i][q + k : q + k + 1, :], shape) for k in range(GROUP)]
        piv = {
            (k, l): jnp.broadcast_to(rows[k][:, first + l : first + l + 1], shape)
            for k in range(GROUP)
            for l in range(k, GROUP)
        }
        scale, inv, mult = [], [], {}
        for k in range(GROUP):
            s = lax.rsqrt(piv[k, k])
            logs = logs + jnp.log(piv[k, k])
            scale.append(s)
            inv.append(s * s)
            for l in range(k + 1, GROUP):
                mult[l, k] = piv[k, l] * inv[k]
            for l in range(k + 1, GROUP):
                for m in range(l, GROUP):
                    piv[l, m] = piv[l, m] - mult[l, k] * piv[k, m]
            for l in range(k + 1, GROUP):
                rows[l] = rows[l] - mult[l, k] * rows[k]
                wrows[l] = wrows[l] - mult[l, k] * wrows[k]
        for k in range(GROUP):
            w_ref[base + i, q + k : q + k + 1, :] = (wrows[k] * scale[k])[0:1, :]
        start = i if q + GROUP < SUB else i + 1
        if start >= TILES:
            continue
        ya = [rows[k] * inv[k] for k in range(GROUP)]
        yw = [wrows[k] * inv[k] for k in range(GROUP)]
        for k in range(GROUP - 1, 0, -1):
            for l in range(k):
                ya[l] = ya[l] - mult[k, l] * ya[k]
                yw[l] = yw[l] - mult[k, l] * yw[k]
        for t in range(start, TILES):
            cols = [jnp.broadcast_to(a[t][:, first + k : first + k + 1], shape) for k in range(GROUP)]
            da = (cols[0] * ya[0] + cols[1] * ya[1]) + (cols[2] * ya[2] + cols[3] * ya[3])
            dw = (cols[0] * yw[0] + cols[1] * yw[1]) + (cols[2] * yw[2] + cols[3] * yw[3])
            a[t] = a[t] - da
            w[t] = w[t] - dw
    return logs


def mm(x, y, dims):
    return lax.dot_general(
        x, y, (dims, ((), ())), precision=lax.Precision.HIGHEST, preferred_element_type=jnp.float32
    )


def panels_body(first, last, count, a_in, w_in, log_in, a, w, log):
    def get(ref, b):
        return ref[b * TILES : (b + 1) * TILES].reshape(LANES, LANES)

    def put(ref, b, value):
        ref[b * TILES : (b + 1) * TILES] = value.reshape(TILES, SUB, LANES)

    a[...] = a_in[...]
    w[...] = w_in[...]
    log[...] = log_in[...]

    def step(k, carry):
        base = TILES * (k * count - (k * (k - 1)) // 2)
        log[...] = log[...] + leaf(a, w, base)
        for kk in range(first, last):

            @pl.when(k == kk)
            def _():
                inv = get(w, block_index(kk, kk, count))
                right = list(range(kk + 1, count))
                left = list(range(kk))
                src = [get(a, block_index(kk, j, count)) for j in right]
                src += [get(w, block_index(j, kk, count)) for j in left]
                if not src:
                    return
                out = mm(inv, jnp.concatenate(src, axis=1), ((1,), (0,)))
                parts = [out[:, n * LANES : (n + 1) * LANES] for n in range(len(src))]
                upper = dict(zip(right, parts[: len(right)]))
                lower = dict(zip(left, parts[len(right) :]))
                for j in left:
                    put(w, block_index(j, kk, count), lower[j])
                lower[kk] = inv
                for i in right:
                    cols = [upper[j] for j in right if j >= i] + [lower[j] for j in range(kk + 1)]
                    upd = mm(upper[i], jnp.concatenate(cols, axis=1), ((0,), (0,)))
                    n = 0
                    for j in right:
                        if j >= i:
                            b = block_index(i, j, count)
                            put(a, b, get(a, b) - upd[:, n * LANES : (n + 1) * LANES])
                            n += 1
                    for j in range(kk + 1):
                        b = block_index(j, i, count)
                        old = get(w, b) if j < kk else jnp.zeros((LANES, LANES), jnp.float32)
                        put(w, b, old - upd[:, n * LANES : (n + 1) * LANES])
                        n += 1

        return carry

    lax.fori_loop(first, last, step, 0)


def panels(first, last, count, a, w, log):
    def body(a_in, w_in, log_in, a_out, w_out, log_out):
        panels_body(first, last, count, a_in, w_in, log_in, a_out, w_out, log_out)

    shapes = [jax.ShapeDtypeStruct(x.shape, jnp.float32) for x in (a, w, log)]
    return pl.pallas_call(body, out_shape=shapes, name=f"panels_{first}")(a, w, log)


def spread_from_first(value, axis):
    size = lax.axis_size(axis)
    index = lax.axis_index(axis)
    stride = 1
    while stride < size:
        stride *= 2
    stride //= 2
    while stride >= 1:
        step = 2 * stride
        pairs = [(s, s + stride) for s in range(0, size, step) if s + stride < size]
        got = lax.ppermute(value, axis, pairs)
        value = jnp.where(index % step == stride, got, value)
        stride //= 2
    return value


def per_device(block):
    width, cols = block.shape
    both = ("row", "col")
    rows_n = lax.axis_size("row")
    devices = rows_n * lax.axis_size("col")
    row = lax.axis_index("row")
    col = lax.axis_index("col")
    count = width // LANES

    packed = jnp.stack(
        [
            block[k * LANES : (k + 1) * LANES, j * LANES : (j + 1) * LANES]
            for k in range(count)
            for j in range(k, count)
        ]
    ).reshape(-1, SUB, LANES)
    tiles = packed.shape[0]
    per = -(-tiles // devices)
    sent = jnp.pad(packed, ((0, per * devices - tiles), (0, 0), (0, 0)))
    sent = sent.reshape(devices, per, SUB, LANES)
    mine = lax.all_to_all(sent, both, 0, 0)[0]
    diag = lax.all_gather(mine, both, axis=0, tiled=True)[:tiles]

    tied, diag = lax.optimization_barrier((block, diag))
    own = spread_from_first(tied[:, :width], "col")
    piece_rows = width // rows_n
    piece = tied[:piece_rows]
    for t in range(1, rows_n):
        got = lax.ppermute(tied[t * piece_rows : (t + 1) * piece_rows], "row", [(0, t)])
        piece = jnp.where(row == t, got, piece)

    log = jnp.zeros((SUB, LANES), jnp.float32)
    half = (count + 1) // 2
    a, w, log = panels(0, half, count, diag, jnp.zeros_like(diag), log)
    piece, own, a = lax.optimization_barrier((piece, own, a))

    top = jnp.zeros((rows_n, piece_rows, cols), jnp.float32)
    top = lax.dynamic_update_slice(top, piece[None], (row, 0, 0))
    for s in range(1, rows_n):
        got = lax.ppermute(piece, "row", [(i, (i + s) % rows_n) for i in range(rows_n)])
        top = lax.dynamic_update_slice(top, got[None], ((row - s) % rows_n, 0, 0))
    top = top.reshape(width, cols)

    a, w, log = panels(half, count, count, a, w, log)
    w_blocks = w.reshape(-1, LANES, LANES)
    zero = jnp.zeros((LANES, LANES), jnp.float32)
    inverse = jnp.concatenate(
        [
            jnp.concatenate(
                [w_blocks[block_index(j, i, count)] if j <= i else zero for j in range(count)], axis=1
            )
            for i in range(count)
        ],
        axis=0,
    )
    high = lax.Precision.HIGH
    panel = lax.dot_general(own, inverse, (((1,), (1,)), ((), ())), precision=high)
    upper = jnp.dot(inverse, top, precision=high)
    update = jnp.dot(panel, upper, precision=high)
    col_block = (cols // width) * col + jnp.arange(cols, dtype=jnp.int32) // width
    first_col = (col_block == 0)[None, :]
    in_row = jnp.arange(width, dtype=jnp.int32)
    keep = (row > 0) | (in_row[:, None] >= in_row[None, :])
    panel = jnp.where(keep, panel, 0.0)
    panel = jnp.concatenate([panel] * (cols // width), axis=1)
    rest = jnp.where(row > 0, block - update, 0.0)
    return jnp.where(first_col, panel, rest), log[0, 0]


def solution(mesh):
    return jax.shard_map(
        per_device,
        mesh=mesh,
        in_specs=(P("row", "col"),),
        out_specs=(P("row", "col"), P()),
        check_vma=False,
    )
```

profile of v0, /device:TPU:0, one launch (start us, length us, event | category | flops | bytes accessed | tf_op | source)
XLA Modules:
  0.0 178.9 jit_solution(9064529820040235622)
XLA Ops:
  0.6 1.0 bitcast_dynamic-update-slice_fusion.17
  1.6 0.8 bitcast_dynamic-update-slice_fusion.16
  2.5 0.8 bitcast_dynamic-update-slice_fusion.15
  5.9 0.8 bitcast_dynamic-update-slice_fusion.11
  9.2 25.1 %all_to_all.5 = f32[32,5,8,128]{3,2,1,0:T(8,128)S(1)} all-to-all(f32[32,5,8,128]{3,2,1,0:T(8,128)S(1)} %bitcast.68), channel_id=1, replica_groups=mesh['row'=8,'col'=4] {'row','col'}, dimensions={0} | all-to-all | bytes 1310720 | tf_op jit(solution)/shard_map/all_to_all | solution.py:170
  34.3 43.7 %all-gather = f32[1,160,8,128]{3,2,0,1:T(8,128)} all-gather(f32[1,5,8,128]{3,2,0,1:T(8,128)S(1)} %slice_bitcast_fusion.10), channel_id=2, replica_groups=mesh['row'=8,'col'=4] {'row','col'}, dimensions={1}, use_global_device_ids=true | all-gather | bytes 675840 | tf_op jit(solution)/shard_map/all_gather | solution.py:171
  78.2 2.3 %collective-permute-start.7 = (f32[512,512]{1,0:T(8,128)S(1)}, f32[512,512]{1,0:T(8,128)}, u32[]{:S(2)}, u32[]{:S(2)}) collective-permute-start(f32[512,512]{1,0:T(8,128)S(1)} %slice.122), channel_id=1, source_target_pairs={{0,2},{4,6},{8,10},{12,14},{16,18},{20,22},{24,26},{28,30}} | collective-permute-start | bytes 3145736 | tf_op jit(solution)/shard_map/ppermute | solution.py:144
  80.5 11.3 %collective-permute-done.7 = f32[512,512]{1,0:T(8,128)} collective-permute-done((f32[512,512]{1,0:T(8,128)S(1)}, f32[512,512]{1,0:T(8,128)}, u32[]{:S(2)}, u32[]{:S(2)}) %collective-permute-start.7) | collective-permute-done | bytes 1048608 | tf_op jit(solution)/shard_map/ppermute | solution.py:144
  92.0 2.3 %collective-permute-start.8 = (f32[512,512]{1,0:T(8,128)S(1)}, f32[512,512]{1,0:T(8,128)}, u32[]{:S(2)}, u32[]{:S(2)}) collective-permute-start(f32[512,512]{1,0:T(8,128)S(1)} %broadcast_select_fusion), channel_id=1, source_target_pairs={{0,1},{2,3},{4,5},{6,7},{8,9},{10,11},{12,13},{14,15},{16,17},{18,... | collective-permute-start | bytes 3145736 | tf_op jit(solution)/shard_map/ppermute | solution.py:144
  94.3 0.9 fusion.13
  95.3 3.1 %collective-permute-start = (f32[64,1024]{1,0:T(8,128)S(1)}, f32[64,1024]{1,0:T(8,128)}, u32[]{:S(2)}, u32[]{:S(2)}) collective-permute-start(f32[64,1024]{1,0:T(8,128)S(1)} %get-tuple-element.34), channel_id=1, source_target_pairs={{0,28},{1,29},{2,30},{3,31}} | collective-permute-start | bytes 786440 | tf_op jit(solution)/shard_map/ppermute | solution.py:178
  98.4 2.0 %collective-permute-start.1 = (f32[64,1024]{1,0:T(8,128)S(1)}, f32[64,1024]{1,0:T(8,128)}, u32[]{:S(2)}, u32[]{:S(2)}) collective-permute-start(f32[64,1024]{1,0:T(8,128)S(1)} %get-tuple-element.33), channel_id=1, source_target_pairs={{0,24},{1,25},{2,26},{3,27}} | collective-permute-start | bytes 786440 | tf_op jit(solution)/shard_map/ppermute | solution.py:178
  100.4 2.0 %collective-permute-start.2 = (f32[64,1024]{1,0:T(8,128)S(1)}, f32[64,1024]{1,0:T(8,128)}, u32[]{:S(2)}, u32[]{:S(2)}) collective-permute-start(f32[64,1024]{1,0:T(8,128)S(1)} %get-tuple-element.32), channel_id=1, source_target_pairs={{0,20},{1,21},{2,22},{3,23}} | collective-permute-start | bytes 786440 | tf_op jit(solution)/shard_map/ppermute | solution.py:178
  102.4 2.0 %collective-permute-start.3 = (f32[64,1024]{1,0:T(8,128)}, f32[64,1024]{1,0:T(8,128)}, u32[]{:S(2)}, u32[]{:S(2)}) collective-permute-start(f32[64,1024]{1,0:T(8,128)} %get-tuple-element.31), channel_id=1, source_target_pairs={{0,16},{1,17},{2,18},{3,19}} | collective-permute-start | bytes 786440 | tf_op jit(solution)/shard_map/ppermute | solution.py:178
  104.4 2.0 %collective-permute-start.4 = (f32[64,1024]{1,0:T(8,128)}, f32[64,1024]{1,0:T(8,128)}, u32[]{:S(2)}, u32[]{:S(2)}) collective-permute-start(f32[64,1024]{1,0:T(8,128)} %get-tuple-element.30), channel_id=1, source_target_pairs={{0,12},{1,13},{2,14},{3,15}} | collective-permute-start | bytes 786440 | tf_op jit(solution)/shard_map/ppermute | solution.py:178
  106.8 2.0 %collective-permute-start.5 = (f32[64,1024]{1,0:T(8,128)}, f32[64,1024]{1,0:T(8,128)}, u32[]{:S(2)}, u32[]{:S(2)}) collective-permute-start(f32[64,1024]{1,0:T(8,128)} %get-tuple-element.29), channel_id=1, source_target_pairs={{0,8},{1,9},{2,10},{3,11}} | collective-permute-start | bytes 786440 | tf_op jit(solution)/shard_map/ppermute | solution.py:178
  109.6 2.0 %collective-permute-start.6 = (f32[64,1024]{1,0:T(8,128)S(1)}, f32[64,1024]{1,0:T(8,128)}, u32[]{:S(2)}, u32[]{:S(2)}) collective-permute-start(f32[64,1024]{1,0:T(8,128)S(1)} %get-tuple-element.28), channel_id=1, source_target_pairs={{0,4},{1,5},{2,6},{3,7}} | collective-permute-start | bytes 786440 | tf_op jit(solution)/shard_map/ppermute | solution.py:178
  111.6 1.8 %copy.10 = f32[512,1024]{0,1:T(8,128)} copy(f32[512,1024]{1,0:T(8,128)S(1)} %copy-done) | data formatting | bytes 4194304 | tf_op args[0]
  113.4 0.9 broadcast_in_dim.56.w_in
  114.9 18.0 %panels_0.1 = (f32[160,8,128]{2,1,0:T(8,128)}, f32[160,8,128]{2,1,0:T(8,128)}, f32[8,128]{1,0:T(8,128)}) custom-call(f32[160,8,128]{2,1,0:T(8,128)} %bitcast.66, f32[160,8,128]{2,1,0:T(8,128)} %broadcast_in_dim.56.w_in, f32[8,128]{1,0:T(8,128)} %broadcast_in_dim.57.log_in), custom_call_target="tpu_custom_call" | custom-call | tf_op jit(solution)/shard_map/panels_0/pallas_call | solution.py:131
  133.5 5.2 %collective-permute-start.11 = (f32[64,1024]{1,0:T(8,128)S(1)}, f32[64,1024]{1,0:T(8,128)S(1)}, u32[]{:S(2)}, u32[]{:S(2)}) collective-permute-start(f32[64,1024]{1,0:T(8,128)S(1)} %select_select_fusion), channel_id=1, source_target_pairs={{0,12},{4,16},{8,20},{12,24},{16,28},{20,0},{24,4},{28,8},{1,13},{... | collective-permute-start | bytes 786440 | tf_op jit(solution)/shard_map/ppermute | solution.py:189
  138.8 3.8 %collective-permute-start.13 = (f32[64,1024]{1,0:T(8,128)S(1)}, f32[64,1024]{1,0:T(8,128)S(1)}, u32[]{:S(2)}, u32[]{:S(2)}) collective-permute-start(f32[64,1024]{1,0:T(8,128)S(1)} %select_select_fusion), channel_id=1, source_target_pairs={{0,20},{4,24},{8,28},{12,0},{16,4},{20,8},{24,12},{28,16},{1,21},{... | collective-permute-start | bytes 786440 | tf_op jit(solution)/shard_map/ppermute | solution.py:189
  142.5 17.1 %panels_2.1 = (f32[160,8,128]{2,1,0:T(8,128)}, f32[160,8,128]{2,1,0:T(8,128)}, f32[8,128]{1,0:T(8,128)}) custom-call(f32[160,8,128]{2,1,0:T(8,128)} %get-tuple-element.16.a_in, f32[160,8,128]{2,1,0:T(8,128)} %get-tuple-element.17.w_in, f32[8,128]{1,0:T(8,128)} %get-tuple-element.18.log_in), custom_call_target="tpu_custom_call" | custom-call | tf_op jit(solution)/shard_map/panels_2/pallas_call | solution.py:131
  159.6 1.2 slice_bitcast_fusion.8
  160.8 1.0 fusion.3
  162.1 1.2 slice.133
  163.3 2.9 %collective-permute-start.14 = (f32[64,1024]{1,0:T(8,128)S(1)}, f32[64,1024]{1,0:T(8,128)S(1)}, u32[]{:S(2)}, u32[]{:S(2)}) collective-permute-start(f32[64,1024]{1,0:T(8,128)S(1)} %select_select_fusion), channel_id=1, source_target_pairs={{0,24},{4,28},{8,0},{12,4},{16,8},{20,12},{24,16},{28,20},{1,25},{... | collective-permute-start | bytes 786440 | tf_op jit(solution)/shard_map/ppermute | solution.py:189
  166.5 3.6 %collective-permute-done.14 = f32[64,1024]{1,0:T(8,128)S(1)} collective-permute-done((f32[64,1024]{1,0:T(8,128)S(1)}, f32[64,1024]{1,0:T(8,128)S(1)}, u32[]{:S(2)}, u32[]{:S(2)}) %collective-permute-start.14) | collective-permute-done | bytes 262176 | tf_op jit(solution)/shard_map/ppermute | solution.py:189
  170.2 2.8 %collective-permute-done.15 = f32[64,1024]{1,0:T(8,128)S(1)} collective-permute-done((f32[64,1024]{1,0:T(8,128)S(1)}, f32[64,1024]{1,0:T(8,128)S(1)}, u32[]{:S(2)}, u32[]{:S(2)}) %collective-permute-start.15) | collective-permute-done | bytes 262176 | tf_op jit(solution)/shard_map/ppermute | solution.py:189
  173.0 1.9 %fusion.9 = f32[512,1024]{1,0:T(8,128)S(1)} fusion(f32[512,1024]{1,0:T(8,128)S(1)} %bitcast.67, f32[128,128]{1,0:T(8,128)S(1)} %get-tuple-element.44, f32[128,128]{1,0:T(8,128)S(1)} %get-tuple-element.36, f32[128,128]{1,0:T(8,128)S(1)} %get-tuple-element.37, f32[128,128]{1,0:T(8,128)S(1)} %get-tuple-element.38, f32[128,128]{1,0:T(8,128)S(1)} %get-tuple-element.39, ...), kind=kOutput, calls=%fused_computation.49 | convolution fusion | flops 1614020608 | bytes 5046272 | tf_op jit(solution)/shard_map/dot_general | solution.py:207
  174.9 2.2 %maximum_select_fusion = f32[512,1024]{0,1:T(8,128)S(1)} fusion(f32[512,512]{0,1:T(8,128)S(1)} %get-tuple-element.45, f32[512,1024]{0,1:T(8,128)S(1)} %copy-done.1, f32[512,512]{0,1:T(8,128)S(1)} %get-tuple-element.46, f32[512,1024]{1,0:T(8,128)S(1)} %fusion.9, pred[1024]{0:T(1024)(128)(4,1)S(1)} %fusion.5, pred[]{:T(512)S(6)} %gt.4), kind=kOutput, calls=%fused_computation | convolution fusion | flops 1612709888 | bytes 8389633 | tf_op jit(solution)/shard_map/dot_general | solution.py:208
  177.1 1.8 %copy.12 = f32[512,1024]{1,0:T(8,128)} copy(f32[512,1024]{0,1:T(8,128)S(1)} %maximum_select_fusion) | data formatting | bytes 4194304
  (45 shorter events, 8.3 us)
Async XLA Ops:
  0.6 77.5 %copy-start = (f32[512,1024]{1,0:T(8,128)S(1)}, f32[512,1024]{1,0:T(8,128)}, u32[]{:S(2)}) copy-start(f32[512,1024]{1,0:T(8,128)} %param.1) | copy-start | bytes 6291460
  78.2 13.6 %collective-permute-start.7 = (f32[512,512]{1,0:T(8,128)S(1)}, f32[512,512]{1,0:T(8,128)}, u32[]{:S(2)}, u32[]{:S(2)}) collective-permute-start(f32[512,512]{1,0:T(8,128)S(1)} %slice.122), channel_id=1, source_target_pairs={{0,2},{4,6},{8,10},{12,14},{16,18},{20,22},{24,26},{28,30}} | collective-permute-start | bytes 3145736 | tf_op jit(solution)/shard_map/ppermute | solution.py:144
  92.0 41.1 %collective-permute-start.8 = (f32[512,512]{1,0:T(8,128)S(1)}, f32[512,512]{1,0:T(8,128)}, u32[]{:S(2)}, u32[]{:S(2)}) collective-permute-start(f32[512,512]{1,0:T(8,128)S(1)} %broadcast_select_fusion), channel_id=1, source_target_pairs={{0,1},{2,3},{4,5},{6,7},{8,9},{10,11},{12,13},{14,15},{16,17},{18,... | collective-permute-start | bytes 3145736 | tf_op jit(solution)/shard_map/ppermute | solution.py:144
  95.3 9.1 %collective-permute-start = (f32[64,1024]{1,0:T(8,128)S(1)}, f32[64,1024]{1,0:T(8,128)}, u32[]{:S(2)}, u32[]{:S(2)}) collective-permute-start(f32[64,1024]{1,0:T(8,128)S(1)} %get-tuple-element.34), channel_id=1, source_target_pairs={{0,28},{1,29},{2,30},{3,31}} | collective-permute-start | bytes 786440 | tf_op jit(solution)/shard_map/ppermute | solution.py:178
  98.4 8.4 %collective-permute-start.1 = (f32[64,1024]{1,0:T(8,128)S(1)}, f32[64,1024]{1,0:T(8,128)}, u32[]{:S(2)}, u32[]{:S(2)}) collective-permute-start(f32[64,1024]{1,0:T(8,128)S(1)} %get-tuple-element.33), channel_id=1, source_target_pairs={{0,24},{1,25},{2,26},{3,27}} | collective-permute-start | bytes 786440 | tf_op jit(solution)/shard_map/ppermute | solution.py:178
  100.4 9.2 %collective-permute-start.2 = (f32[64,1024]{1,0:T(8,128)S(1)}, f32[64,1024]{1,0:T(8,128)}, u32[]{:S(2)}, u32[]{:S(2)}) collective-permute-start(f32[64,1024]{1,0:T(8,128)S(1)} %get-tuple-element.32), channel_id=1, source_target_pairs={{0,20},{1,21},{2,22},{3,23}} | collective-permute-start | bytes 786440 | tf_op jit(solution)/shard_map/ppermute | solution.py:178
  102.4 30.5 %collective-permute-start.3 = (f32[64,1024]{1,0:T(8,128)}, f32[64,1024]{1,0:T(8,128)}, u32[]{:S(2)}, u32[]{:S(2)}) collective-permute-start(f32[64,1024]{1,0:T(8,128)} %get-tuple-element.31), channel_id=1, source_target_pairs={{0,16},{1,17},{2,18},{3,19}} | collective-permute-start | bytes 786440 | tf_op jit(solution)/shard_map/ppermute | solution.py:178
  104.4 28.5 %collective-permute-start.4 = (f32[64,1024]{1,0:T(8,128)}, f32[64,1024]{1,0:T(8,128)}, u32[]{:S(2)}, u32[]{:S(2)}) collective-permute-start(f32[64,1024]{1,0:T(8,128)} %get-tuple-element.30), channel_id=1, source_target_pairs={{0,12},{1,13},{2,14},{3,15}} | collective-permute-start | bytes 786440 | tf_op jit(solution)/shard_map/ppermute | solution.py:178
  106.8 26.1 %collective-permute-start.5 = (f32[64,1024]{1,0:T(8,128)}, f32[64,1024]{1,0:T(8,128)}, u32[]{:S(2)}, u32[]{:S(2)}) collective-permute-start(f32[64,1024]{1,0:T(8,128)} %get-tuple-element.29), channel_id=1, source_target_pairs={{0,8},{1,9},{2,10},{3,11}} | collective-permute-start | bytes 786440 | tf_op jit(solution)/shard_map/ppermute | solution.py:178
  109.6 23.3 %collective-permute-start.6 = (f32[64,1024]{1,0:T(8,128)S(1)}, f32[64,1024]{1,0:T(8,128)}, u32[]{:S(2)}, u32[]{:S(2)}) collective-permute-start(f32[64,1024]{1,0:T(8,128)S(1)} %get-tuple-element.28), channel_id=1, source_target_pairs={{0,4},{1,5},{2,6},{3,7}} | collective-permute-start | bytes 786440 | tf_op jit(solution)/shard_map/ppermute | solution.py:178
  133.4 29.9 %collective-permute-start.9 = (f32[64,1024]{1,0:T(8,128)S(1)}, f32[64,1024]{1,0:T(8,128)S(1)}, u32[]{:S(2)}, u32[]{:S(2)}) collective-permute-start(f32[64,1024]{1,0:T(8,128)S(1)} %select_select_fusion), channel_id=1, source_target_pairs={{0,4},{4,8},{8,12},{12,16},{16,20},{20,24},{24,28},{28,0},{1,5},{5... | collective-permute-start | bytes 786440 | tf_op jit(solution)/shard_map/ppermute | solution.py:189
  133.5 32.8 %collective-permute-start.10 = (f32[64,1024]{1,0:T(8,128)S(1)}, f32[64,1024]{1,0:T(8,128)S(1)}, u32[]{:S(2)}, u32[]{:S(2)}) collective-permute-start(f32[64,1024]{1,0:T(8,128)S(1)} %select_select_fusion), channel_id=1, source_target_pairs={{0,8},{4,12},{8,16},{12,20},{16,24},{20,28},{24,0},{28,4},{1,9},{5... | collective-permute-start | bytes 786440 | tf_op jit(solution)/shard_map/ppermute | solution.py:189
  133.5 32.9 %collective-permute-start.11 = (f32[64,1024]{1,0:T(8,128)S(1)}, f32[64,1024]{1,0:T(8,128)S(1)}, u32[]{:S(2)}, u32[]{:S(2)}) collective-permute-start(f32[64,1024]{1,0:T(8,128)S(1)} %select_select_fusion), channel_id=1, source_target_pairs={{0,12},{4,16},{8,20},{12,24},{16,28},{20,0},{24,4},{28,8},{1,13},{... | collective-permute-start | bytes 786440 | tf_op jit(solution)/shard_map/ppermute | solution.py:189
  138.8 27.7 %collective-permute-start.12 = (f32[64,1024]{1,0:T(8,128)S(1)}, f32[64,1024]{1,0:T(8,128)S(1)}, u32[]{:S(2)}, u32[]{:S(2)}) collective-permute-start(f32[64,1024]{1,0:T(8,128)S(1)} %select_select_fusion), channel_id=1, source_target_pairs={{0,16},{4,20},{8,24},{12,28},{16,0},{20,4},{24,8},{28,12},{1,17},{... | collective-permute-start | bytes 786440 | tf_op jit(solution)/shard_map/ppermute | solution.py:189
  138.8 27.7 %collective-permute-start.13 = (f32[64,1024]{1,0:T(8,128)S(1)}, f32[64,1024]{1,0:T(8,128)S(1)}, u32[]{:S(2)}, u32[]{:S(2)}) collective-permute-start(f32[64,1024]{1,0:T(8,128)S(1)} %select_select_fusion), channel_id=1, source_target_pairs={{0,20},{4,24},{8,28},{12,0},{16,4},{20,8},{24,12},{28,16},{1,21},{... | collective-permute-start | bytes 786440 | tf_op jit(solution)/shard_map/ppermute | solution.py:189
  163.3 6.8 %collective-permute-start.14 = (f32[64,1024]{1,0:T(8,128)S(1)}, f32[64,1024]{1,0:T(8,128)S(1)}, u32[]{:S(2)}, u32[]{:S(2)}) collective-permute-start(f32[64,1024]{1,0:T(8,128)S(1)} %select_select_fusion), channel_id=1, source_target_pairs={{0,24},{4,28},{8,0},{12,4},{16,8},{20,12},{24,16},{28,20},{1,25},{... | collective-permute-start | bytes 786440 | tf_op jit(solution)/shard_map/ppermute | solution.py:189
  166.3 6.7 %collective-permute-start.15 = (f32[64,1024]{1,0:T(8,128)S(1)}, f32[64,1024]{1,0:T(8,128)S(1)}, u32[]{:S(2)}, u32[]{:S(2)}) collective-permute-start(f32[64,1024]{1,0:T(8,128)S(1)} %select_select_fusion), channel_id=1, source_target_pairs={{0,28},{4,0},{8,4},{12,8},{16,12},{20,16},{24,20},{28,24},{1,29},{... | collective-permute-start | bytes 786440 | tf_op jit(solution)/shard_map/ppermute | solution.py:189
  173.0 1.9 %copy-start.1 = (f32[512,1024]{0,1:T(8,128)S(1)}, f32[512,1024]{0,1:T(8,128)}, u32[]{:S(2)}) copy-start(f32[512,1024]{0,1:T(8,128)} %copy.10) | copy-start | bytes 6291460
where the time goes:
time: 180 us; the launch traced here: 179 us
  blocking collectives  68.9 us (38%)
  Pallas kernels  35.1 us (20%)
  starting transfers between devices  31.8 us (18%)
  waiting for transfers between devices  19 us (11%)
  local copies, waits for them, and re-layouts  17.5 us (10%)
  matrix products  5.15 us (3%)
    all_gather x1, blocking collectives, per_device(): diag = lax.all_gather(mine, both, axis=0, tiled=True)[:tiles]  43.7 us
    pallas_call x2, Pallas kernels, panels(): pl.pallas_call(body, out_shape=shapes, name=f'panels_{first}')(a, w, log)  35.1 us
    all_to_all x1, blocking collectives, per_device(): mine = lax.all_to_all(sent, both, 0, 0)[0]  25.1 us
    ppermute x7, starting transfers between devices, per_device(): lax.ppermute(tied[t * piece_rows:(t + 1) * piece_rows], 'row', [(0, t)])  15.1 us
    ppermute x7, starting transfers between devices, per_device(): lax.ppermute(piece, 'row', [(i, (i + s) % rows_n) for i in range(rows_n)])  12.1 us
    unnamed x15, local copies, waits for them, and re-layouts  11.4 us
    ppermute x2, waiting for transfers between devices, spread_from_first(): got = lax.ppermute(value, axis, pairs)  11.3 us
    ppermute x7, waiting for transfers between devices, per_device(): lax.ppermute(piece, 'row', [(i, (i + s) % rows_n) for i in range(rows_n)])  6.43 us
  transfers between devices with their start and end apart: 16, of which 5 were waited for; matrix products, arithmetic and copies ran while one was open for 5% of the time, Pallas kernels for 20%

commit v1 on v0

v1 whole, which is shorter than its diff:
```python
import jax
import jax.numpy as jnp
from jax import lax
from jax.experimental import pallas as pl
from jax.experimental.pallas import tpu as pltpu
from jax.sharding import PartitionSpec as P

LANES = 128
SUB = 8
TILES = LANES // SUB
GROUP = 4


def block_index(k, j, count):
    return k * count - (k * (k - 1)) // 2 + (j - k)


def leaf(a_ref, w_ref, base):
    a = [a_ref[base + t] for t in range(TILES)]
    sub = lax.broadcasted_iota(jnp.int32, (SUB, LANES), 0)
    lane = lax.broadcasted_iota(jnp.int32, (SUB, LANES), 1)
    w = [jnp.where(lane == sub + SUB * t, 1.0, 0.0).astype(jnp.float32) for t in range(TILES)]
    logs = jnp.zeros((SUB, LANES), jnp.float32)
    shape = (SUB, LANES)
    for g in range(LANES // GROUP):
        i, q, first = (GROUP * g) // SUB, (GROUP * g) % SUB, GROUP * g
        rows = [jnp.broadcast_to(a[i][q + k : q + k + 1, :], shape) for k in range(GROUP)]
        wrows = [jnp.broadcast_to(w[i][q + k : q + k + 1, :], shape) for k in range(GROUP)]
        piv = {
            (k, l): jnp.broadcast_to(rows[k][:, first + l : first + l + 1], shape)
            for k in range(GROUP)
            for l in range(k, GROUP)
        }
        scale, inv, mult = [], [], {}
        for k in range(GROUP):
            s = lax.rsqrt(piv[k, k])
            logs = logs + jnp.log(piv[k, k])
            scale.append(s)
            inv.append(s * s)
            for l in range(k + 1, GROUP):
                mult[l, k] = piv[k, l] * inv[k]
            for l in range(k + 1, GROUP):
                for m in range(l, GROUP):
                    piv[l, m] = piv[l, m] - mult[l, k] * piv[k, m]
            for l in range(k + 1, GROUP):
                rows[l] = rows[l] - mult[l, k] * rows[k]
                wrows[l] = wrows[l] - mult[l, k] * wrows[k]
        for k in range(GROUP):
            w_ref[base + i, q + k : q + k + 1, :] = (wrows[k] * scale[k])[0:1, :]
        start = i if q + GROUP < SUB else i + 1
        if start >= TILES:
            continue
        ya = [rows[k] * inv[k] for k in range(GROUP)]
        yw = [wrows[k] * inv[k] for k in range(GROUP)]
        for k in range(GROUP - 1, 0, -1):
            for l in range(k):
                ya[l] = ya[l] - mult[k, l] * ya[k]
                yw[l] = yw[l] - mult[k, l] * yw[k]
        for t in range(start, TILES):
            cols = [jnp.broadcast_to(a[t][:, first + k : first + k + 1], shape) for k in range(GROUP)]
            da = (cols[0] * ya[0] + cols[1] * ya[1]) + (cols[2] * ya[2] + cols[3] * ya[3])
            dw = (cols[0] * yw[0] + cols[1] * yw[1]) + (cols[2] * yw[2] + cols[3] * yw[3])
            a[t] = a[t] - da
            w[t] = w[t] - dw
    return logs


def mm(x, y, dims):
    return lax.dot_general(
        x, y, (dims, ((), ())), precision=lax.Precision.HIGHEST, preferred_element_type=jnp.float32
    )


def get(ref, b):
    return ref[b * TILES : (b + 1) * TILES].reshape(LANES, LANES)


def put(ref, b, value):
    ref[b * TILES : (b + 1) * TILES] = value.reshape(TILES, SUB, LANES)


def row_panel(kk, count, a, w):
    inv = get(w, block_index(kk, kk, count))
    right, left = list(range(kk + 1, count)), list(range(kk))
    src = [get(a, block_index(kk, j, count)) for j in right]
    src += [get(w, block_index(j, kk, count)) for j in left]
    if not src:
        return
    out = mm(inv, jnp.concatenate(src, axis=1), ((1,), (0,)))
    for n, j in enumerate(right):
        put(a, block_index(kk, j, count), out[:, n * LANES : (n + 1) * LANES])
    for n, j in enumerate(left, len(right)):
        put(w, block_index(j, kk, count), out[:, n * LANES : (n + 1) * LANES])


def trail(kk, count, a, w):
    for i in range(kk + 1, count):
        cols = [get(a, block_index(kk, j, count)) for j in range(i, count)]
        cols += [get(w, block_index(j, kk, count)) for j in range(kk + 1)]
        upd = mm(get(a, block_index(kk, i, count)), jnp.concatenate(cols, axis=1), ((0,), (0,)))
        n = 0
        for j in range(i, count):
            b = block_index(i, j, count)
            put(a, b, get(a, b) - upd[:, n * LANES : (n + 1) * LANES])
            n += 1
        for j in range(kk + 1):
            b = block_index(j, i, count)
            old = get(w, b) if j < kk else jnp.zeros((LANES, LANES), jnp.float32)
            put(w, b, old - upd[:, n * LANES : (n + 1) * LANES])
            n += 1


def first_panel(top, count):
    def body(top_ref, out, inv, log, a, w):
        for j in range(count):
            put(a, j, top_ref[:, j * LANES : (j + 1) * LANES])
        log[...] = leaf(a, w, 0)
        row_panel(0, count, a, w)
        for j in range(1, count):
            out[:, j * LANES : (j + 1) * LANES] = get(a, j)
        out[:, :LANES] = jnp.zeros((LANES, LANES), jnp.float32)
        inv[...] = get(w, 0)

    f32 = jnp.float32
    return pl.pallas_call(
        body,
        out_shape=[
            jax.ShapeDtypeStruct((LANES, count * LANES), f32),
            jax.ShapeDtypeStruct((LANES, LANES), f32),
            jax.ShapeDtypeStruct((SUB, LANES), f32),
        ],
        scratch_shapes=[
            pltpu.VMEM((count * TILES, SUB, LANES), f32),
            pltpu.VMEM((TILES, SUB, LANES), f32),
        ],
        name="first_panel",
    )(top)


def other_panels(top, inv, log, rest, count):
    blocks = count * (count + 1) // 2

    def body(top_ref, inv_ref, log_ref, rest_ref, inverse, log, a, w):
        for j in range(1, count):
            put(a, j, top_ref[:, j * LANES : (j + 1) * LANES])
        for b in range(count, blocks):
            n = b - count
            put(a, b, rest_ref[:, n * LANES : (n + 1) * LANES])
        put(w, 0, inv_ref[...])
        log[...] = log_ref[...]
        trail(0, count, a, w)

        def step(k, carry):
            base = TILES * (k * count - (k * (k - 1)) // 2)
            log[...] = log[...] + leaf(a, w, base)
            for kk in range(1, count):

                @pl.when(k == kk)
                def _():
                    row_panel(kk, count, a, w)
                    trail(kk, count, a, w)

            return carry

        lax.fori_loop(1, count, step, 0)
        for i in range(count):
            for j in range(count):
                value = get(w, block_index(j, i, count)) if j <= i else jnp.zeros((LANES, LANES), jnp.float32)
                inverse[i * LANES : (i + 1) * LANES, j * LANES : (j + 1) * LANES] = value

    f32 = jnp.float32
    return pl.pallas_call(
        body,
        out_shape=[
            jax.ShapeDtypeStruct((count * LANES, count * LANES), f32),
            jax.ShapeDtypeStruct((SUB, LANES), f32),
        ],
        scratch_shapes=[
            pltpu.VMEM((blocks * TILES, SUB, LANES), f32),
            pltpu.VMEM((blocks * TILES, SUB, LANES), f32),
        ],
        name="other_panels",
    )(top, inv, log, rest)


def tree_rounds(value, axes, strides):
    index = lax.axis_index(axes)
    size = lax.axis_size(axes)
    have = [0]
    for stride in strides:
        got = lax.ppermute(value, axes, [(s, s + stride) for s in have])
        value = jnp.where((index // stride) % 2 == 1, got, value)
        have = have + [s + stride for s in have]
    assert len(have) == size
    return value


def halvings(size, unit=1):
    out = []
    while size > 1:
        size //= 2
        out.append(size * unit)
    return out


def per_device(block):
    width, cols = block.shape
    both = ("row", "col")
    rows_n, cols_n = lax.axis_size("row"), lax.axis_size("col")
    row = lax.axis_index("row")
    col = lax.axis_index("col")
    count = width // LANES
    per_col = cols // width

    first = block[:LANES, :width]
    rest = jnp.concatenate(
        [block[k * LANES : (k + 1) * LANES, k * LANES : width] for k in range(1, count)], axis=1
    )
    row_strides, col_strides = halvings(rows_n, cols_n), halvings(cols_n)
    first = tree_rounds(first, both, row_strides + col_strides)
    rest = tree_rounds(rest, both, col_strides[:-1] + row_strides[::-1] + col_strides[-1:])

    held = block[:, :width]
    piece_rows = width // rows_n
    pieces = held.reshape(rows_n, piece_rows, width)
    slots = [jnp.zeros((piece_rows, width), jnp.float32) for _ in range(per_col)]
    for s in range(rows_n):
        mine = lax.dynamic_index_in_dim(pieces, (row + s) % rows_n, 0, keepdims=False)
        pairs = [
            (r * cols_n, ((r + s) % rows_n) * cols_n + r // per_col) for r in range(rows_n)
        ]
        got = lax.ppermute(mine, both, pairs)
        slots = [
            jnp.where((row - per_col * col - b) % rows_n == s, got, slots[b]) for b in range(per_col)
        ]
    piece = jnp.stack(slots)[:, None]
    own = tree_rounds(held, "col", col_strides)

    far = jnp.zeros((per_col, rows_n, piece_rows, width), jnp.float32)
    far = lax.dynamic_update_slice(far, piece, (0, row, 0, 0))
    for s in range(1, rows_n):
        got = lax.ppermute(piece, "row", [(i, (i + s) % rows_n) for i in range(rows_n)])
        far = lax.dynamic_update_slice(far, got, (0, (row - s) % rows_n, 0, 0))
    far = far.reshape(cols, width)

    top, inv, log = first_panel(first, count)
    inverse, log = other_panels(top, inv, log, rest, count)

    high = lax.Precision.HIGH
    across = (((1,), (1,)), ((), ()))
    panel = lax.dot_general(own, inverse, across, precision=high)
    other = lax.dot_general(far, inverse, across, precision=high)
    update = lax.dot_general(panel, other, across, precision=high)
    col_block = per_col * col + jnp.arange(cols, dtype=jnp.int32) // width
    first_col = (col_block == 0)[None, :]
    in_row = jnp.arange(width, dtype=jnp.int32)
    keep = (row > 0) | (in_row[:, None] >= in_row[None, :])
    panel = jnp.where(keep, panel, 0.0)
    panel = jnp.concatenate([panel] * per_col, axis=1)
    rest_out = jnp.where(row > 0, block - update, 0.0)
    return jnp.where(first_col, panel, rest_out), log[0, 0]


def solution(mesh):
    return jax.shard_map(
        per_device,
        mesh=mesh,
        in_specs=(P("row", "col"),),
        out_specs=(P("row", "col"), P()),
        check_vma=False,
    )
```

time: 180 us -> 146 us (0.81)
  the two profiles are of different devices: /device:TPU:0 before, /device:TPU:24 now
where the time goes in v1:
time: 146 us
  starting transfers between devices  44.2 us (30%)
  waiting for transfers between devices  39.4 us (27%)
  Pallas kernels  34.2 us (23%)
  local copies, waits for them, and re-layouts  15 us (10%)
  matrix products  6.86 us (5%)
  other arithmetic  4.88 us (3%)
    pallas_call x1, Pallas kernels, other_panels(): pl.pallas_call(body, out_shape=[jax.ShapeDtypeStruct((count * LANES, coun...  25.5 us
    ppermute x7, waiting for transfers between devices, per_device(): lax.ppermute(piece, 'row', [(i, (i + s) % rows_n) for i in range(rows_n)])  20.3 us
    ppermute x12, waiting for transfers between devices, tree_rounds(): got = lax.ppermute(value, axes, [(s, s + stride) for s in have])  19.1 us
    ppermute x8, starting transfers between devices, per_device(): got = lax.ppermute(mine, both, pairs)  17.9 us
    ppermute x12, starting transfers between devices, tree_rounds(): got = lax.ppermute(value, axes, [(s, s + stride) for s in have])  13.3 us
    ppermute x7, starting transfers between devices, per_device(): lax.ppermute(piece, 'row', [(i, (i + s) % rows_n) for i in range(rows_n)])  13 us
    pallas_call x1, Pallas kernels, first_panel(): pl.pallas_call(body, out_shape=[jax.ShapeDtypeStruct((LANES, count * LANE...  8.74 us
    dynamic_update_slice x7, local copies, waits for them, and re-layouts, per_device(): far = lax.dynamic_update_slice(far, got, (0, (row - s) % rows_n, 0, 0))  5.05 us
  transfers between devices with their start and end apart: 27, of which 5 were waited for; matrix products, arithmetic and copies ran while one was open for 13% of the time, Pallas kernels for 23%

profile of v1, /device:TPU:24, one launch (start us, length us, event | category | flops | bytes accessed | tf_op | source)
XLA Modules:
  0.0 145.8 jit_solution(17560428304283043881)
XLA Ops:
  0.7 1.4 slice.18
  3.1 4.3 %collective-permute-start.12 = (f32[64,512]{1,0:T(8,128)S(1)}, f32[64,512]{1,0:T(8,128)}, u32[]{:S(2)}, u32[]{:S(2)}) collective-permute-start(f32[64,512]{1,0:T(8,128)S(1)} %get-tuple-element.23), channel_id=1, source_target_pairs={{0,28},{4,0},{8,5},{12,9},{16,14},{20,18},{24,23},{28,27}} | collective-permute-start | bytes 393224 | tf_op jit(solution)/shard_map/ppermute | solution.py:232
  7.4 1.9 %collective-permute-start.13 = (f32[64,512]{1,0:T(8,128)S(1)}, f32[64,512]{1,0:T(8,128)}, u32[]{:S(2)}, u32[]{:S(2)}) collective-permute-start(f32[64,512]{1,0:T(8,128)S(1)} %get-tuple-element.22), channel_id=1, source_target_pairs={{0,24},{4,28},{8,1},{12,5},{16,10},{20,14},{24,19},{28,23}} | collective-permute-start | bytes 393224 | tf_op jit(solution)/shard_map/ppermute | solution.py:232
  9.4 1.9 %collective-permute-start.14 = (f32[64,512]{1,0:T(8,128)S(1)}, f32[64,512]{1,0:T(8,128)}, u32[]{:S(2)}, u32[]{:S(2)}) collective-permute-start(f32[64,512]{1,0:T(8,128)S(1)} %get-tuple-element.21), channel_id=1, source_target_pairs={{0,20},{4,24},{8,29},{12,1},{16,6},{20,10},{24,15},{28,19}} | collective-permute-start | bytes 393224 | tf_op jit(solution)/shard_map/ppermute | solution.py:232
  11.3 1.9 %collective-permute-start.15 = (f32[64,512]{1,0:T(8,128)}, f32[64,512]{1,0:T(8,128)}, u32[]{:S(2)}, u32[]{:S(2)}) collective-permute-start(f32[64,512]{1,0:T(8,128)} %get-tuple-element.20), channel_id=1, source_target_pairs={{0,16},{4,20},{8,25},{12,29},{16,2},{20,6},{24,11},{28,15}} | collective-permute-start | bytes 393224 | tf_op jit(solution)/shard_map/ppermute | solution.py:232
  13.2 1.9 %collective-permute-start.16 = (f32[64,512]{1,0:T(8,128)}, f32[64,512]{1,0:T(8,128)}, u32[]{:S(2)}, u32[]{:S(2)}) collective-permute-start(f32[64,512]{1,0:T(8,128)} %get-tuple-element.19), channel_id=1, source_target_pairs={{0,12},{4,16},{8,21},{12,25},{16,30},{20,2},{24,7},{28,11}} | collective-permute-start | bytes 393224 | tf_op jit(solution)/shard_map/ppermute | solution.py:232
  15.2 1.9 %collective-permute-start.17 = (f32[64,512]{1,0:T(8,128)}, f32[64,512]{1,0:T(8,128)}, u32[]{:S(2)}, u32[]{:S(2)}) collective-permute-start(f32[64,512]{1,0:T(8,128)} %get-tuple-element.18), channel_id=1, source_target_pairs={{0,8},{4,12},{8,17},{12,21},{16,26},{20,30},{24,3},{28,7}} | collective-permute-start | bytes 393224 | tf_op jit(solution)/shard_map/ppermute | solution.py:232
  17.1 1.9 %collective-permute-start.18 = (f32[64,512]{1,0:T(8,128)}, f32[64,512]{1,0:T(8,128)}, u32[]{:S(2)}, u32[]{:S(2)}) collective-permute-start(f32[64,512]{1,0:T(8,128)} %get-tuple-element.17), channel_id=1, source_target_pairs={{0,4},{4,8},{8,13},{12,17},{16,22},{20,26},{24,31},{28,3}} | collective-permute-start | bytes 393224 | tf_op jit(solution)/shard_map/ppermute | solution.py:232
  19.1 1.9 %collective-permute-start.19 = (f32[64,512]{1,0:T(8,128)}, f32[64,512]{1,0:T(8,128)}, u32[]{:S(2)}, u32[]{:S(2)}) collective-permute-start(f32[64,512]{1,0:T(8,128)} %get-tuple-element.16), channel_id=1, source_target_pairs={{0,0},{4,4},{8,9},{12,13},{16,18},{20,22},{24,27},{28,31}} | collective-permute-start | bytes 393224 | tf_op jit(solution)/shard_map/ppermute | solution.py:232
  21.9 1.8 %copy.6 = f32[512,1024]{0,1:T(8,128)} copy(f32[512,1024]{1,0:T(8,128)S(1)} %copy-done) | data formatting | bytes 4194304 | tf_op args[0]
  23.8 1.4 collective-permute-start
  28.7 8.0 %collective-permute-start.21 = (f32[2,1,64,512]{3,2,1,0:T(8,128)S(1)}, f32[2,1,64,512]{3,2,1,0:T(8,128)S(1)}, u32[]{:S(2)}, u32[]{:S(2)}) collective-permute-start(f32[2,1,64,512]{3,2,1,0:T(8,128)S(1)} %maximum_bitcast_fusion), channel_id=1, source_target_pairs={{0,8},{4,12},{8,16},{12,20},{16,24},{20,28},{24,0},{28,4},{1,9},{5... | collective-permute-start | bytes 786440 | tf_op jit(solution)/shard_map/ppermute | solution.py:242
  36.7 1.6 %broadcast_in_dim.27 = f32[2,8,64,512]{3,2,1,0:T(8,128)} broadcast(f32[]{:T(128)} %constant.280.clone.1), dimensions={} | broadcast | bytes 2097156 | tf_op jit(solution)/shard_map/broadcast_in_dim | solution.py:239
  39.1 4.4 %collective-permute-start.23 = (f32[2,1,64,512]{3,2,1,0:T(8,128)S(1)}, f32[2,1,64,512]{3,2,1,0:T(8,128)S(1)}, u32[]{:S(2)}, u32[]{:S(2)}) collective-permute-start(f32[2,1,64,512]{3,2,1,0:T(8,128)S(1)} %maximum_bitcast_fusion), channel_id=1, source_target_pairs={{0,16},{4,20},{8,24},{12,28},{16,0},{20,4},{24,8},{28,12},{1,17},{... | collective-permute-start | bytes 786440 | tf_op jit(solution)/shard_map/ppermute | solution.py:242
  44.2 1.3 collective-permute-start.3
  47.0 20.3 %collective-permute-done.22 = f32[2,1,64,512]{3,2,1,0:T(8,128)S(1)} collective-permute-done((f32[2,1,64,512]{3,2,1,0:T(8,128)S(1)}, f32[2,1,64,512]{3,2,1,0:T(8,128)S(1)}, u32[]{:S(2)}, u32[]{:S(2)}) %collective-permute-start.22) | collective-permute-done | bytes 262176 | tf_op jit(solution)/shard_map/ppermute | solution.py:242
  68.0 1.3 collective-permute-start.4
  70.8 5.0 %collective-permute-done.4 = f32[128,512]{1,0:T(8,128)S(1)} collective-permute-done((f32[128,512]{1,0:T(8,128)S(1)}, f32[128,512]{1,0:T(8,128)S(1)}, u32[]{:S(2)}, u32[]{:S(2)}) %collective-permute-start.4) | collective-permute-done | bytes 262176 | tf_op jit(solution)/shard_map/ppermute | solution.py:191
  76.5 1.3 collective-permute-start.5
  78.5 1.3 collective-permute-start.10
  79.8 1.8 %collective-permute-done.5 = f32[128,512]{1,0:T(8,128)S(1)} collective-permute-done((f32[128,512]{1,0:T(8,128)S(1)}, f32[128,512]{1,0:T(8,128)S(1)}, u32[]{:S(2)}, u32[]{:S(2)}) %collective-permute-start.5) | collective-permute-done | bytes 262176 | tf_op jit(solution)/shard_map/ppermute | solution.py:191
  81.7 1.3 collective-permute-start.6
  83.2 1.4 collective-permute-start.1
  84.6 12.3 %collective-permute-done.10 = f32[128,768]{1,0:T(8,128)S(1)} collective-permute-done((f32[128,768]{1,0:T(8,128)S(1)}, f32[128,768]{1,0:T(8,128)S(1)}, u32[]{:S(2)}, u32[]{:S(2)}) %collective-permute-start.10) | collective-permute-done | bytes 393248 | tf_op jit(solution)/shard_map/ppermute | solution.py:191
  96.9 1.3 collective-permute-start.11
  100.4 8.7 %first_panel.1 = (f32[128,512]{1,0:T(8,128)}, f32[128,128]{1,0:T(8,128)}, f32[8,128]{1,0:T(8,128)}) custom-call(f32[128,512]{1,0:T(8,128)} %broadcast_select_fusion.10.top_ref), custom_call_target="tpu_custom_call" | custom-call | tf_op jit(solution)/shard_map/first_panel/pallas_call | solution.py:125
  110.0 25.5 %other_panels.1 = (f32[512,512]{1,0:T(8,128)}, f32[8,128]{1,0:T(8,128)}) custom-call(f32[128,512]{1,0:T(8,128)} %get-tuple-element.7.top_ref, f32[128,128]{1,0:T(8,128)} %get-tuple-element.8.inv_ref, f32[8,128]{1,0:T(8,128)} %get-tuple-element.9.log_ref, f32[128,768]{1,0:T(8,128)} %broadcast_select_fusion.5.rest_ref), custom_call_target="tpu_custom_call" | custom-call | tf_op jit(solution)/shard_map/other_panels/pallas_call | solution.py:172
  135.4 1.2 slice.23
  136.6 3.8 %fusion.10 = f32[1024,512]{1,0:T(8,128)S(1)} fusion(f32[1024,512]{1,0:T(8,128)} %bitcast.12, f32[512,512]{1,0:T(8,128)} %get-tuple-element.10), kind=kOutput, calls=%fused_computation.47 | convolution fusion | flops 1610612736 | bytes 5242880 | tf_op jit(solution)/shard_map/dot_general | solution.py:252
  140.5 1.1 fusion.3
  142.0 2.0 %maximum_select_fusion = f32[512,1024]{0,1:T(8,128)S(1)} fusion(f32[512,512]{0,1:T(8,128)S(1)} %get-tuple-element.24, f32[512,1024]{0,1:T(8,128)S(1)} %copy-done.1, f32[512,512]{0,1:T(8,128)S(1)} %get-tuple-element.25, f32[1024,512]{1,0:T(8,128)S(1)} %fusion.10, pred[1024]{0:T(1024)(128)(4,1)S(1)} %fusion.6, pred[]{:T(512)S(6)} %gt.4), kind=kOutput, calls=%fused_computation | convolution fusion | flops 1612709888 | bytes 8389633 | tf_op jit(solution)/shard_map/dot_general | solution.py:253
  144.0 1.8 %copy.8 = f32[512,1024]{1,0:T(8,128)} copy(f32[512,1024]{0,1:T(8,128)S(1)} %maximum_select_fusion) | data formatting | bytes 4194304
  (67 shorter events, 15.6 us)
Async XLA Ops:
  0.7 20.3 %copy-start = (f32[512,1024]{1,0:T(8,128)S(1)}, f32[512,1024]{1,0:T(8,128)}, u32[]{:S(2)}) copy-start(f32[512,1024]{1,0:T(8,128)} %param.1) | copy-start | bytes 6291460
  3.1 12.1 %collective-permute-start.12 = (f32[64,512]{1,0:T(8,128)S(1)}, f32[64,512]{1,0:T(8,128)}, u32[]{:S(2)}, u32[]{:S(2)}) collective-permute-start(f32[64,512]{1,0:T(8,128)S(1)} %get-tuple-element.23), channel_id=1, source_target_pairs={{0,28},{4,0},{8,5},{12,9},{16,14},{20,18},{24,23},{28,27}} | collective-permute-start | bytes 393224 | tf_op jit(solution)/shard_map/ppermute | solution.py:232
  7.4 9.7 %collective-permute-start.13 = (f32[64,512]{1,0:T(8,128)S(1)}, f32[64,512]{1,0:T(8,128)}, u32[]{:S(2)}, u32[]{:S(2)}) collective-permute-start(f32[64,512]{1,0:T(8,128)S(1)} %get-tuple-element.22), channel_id=1, source_target_pairs={{0,24},{4,28},{8,1},{12,5},{16,10},{20,14},{24,19},{28,23}} | collective-permute-start | bytes 393224 | tf_op jit(solution)/shard_map/ppermute | solution.py:232
  9.4 9.8 %collective-permute-start.14 = (f32[64,512]{1,0:T(8,128)S(1)}, f32[64,512]{1,0:T(8,128)}, u32[]{:S(2)}, u32[]{:S(2)}) collective-permute-start(f32[64,512]{1,0:T(8,128)S(1)} %get-tuple-element.21), channel_id=1, source_target_pairs={{0,20},{4,24},{8,29},{12,1},{16,6},{20,10},{24,15},{28,19}} | collective-permute-start | bytes 393224 | tf_op jit(solution)/shard_map/ppermute | solution.py:232
  11.3 12.5 %collective-permute-start.15 = (f32[64,512]{1,0:T(8,128)}, f32[64,512]{1,0:T(8,128)}, u32[]{:S(2)}, u32[]{:S(2)}) collective-permute-start(f32[64,512]{1,0:T(8,128)} %get-tuple-element.20), channel_id=1, source_target_pairs={{0,16},{4,20},{8,25},{12,29},{16,2},{20,6},{24,11},{28,15}} | collective-permute-start | bytes 393224 | tf_op jit(solution)/shard_map/ppermute | solution.py:232
  13.2 11.9 %collective-permute-start.16 = (f32[64,512]{1,0:T(8,128)}, f32[64,512]{1,0:T(8,128)}, u32[]{:S(2)}, u32[]{:S(2)}) collective-permute-start(f32[64,512]{1,0:T(8,128)} %get-tuple-element.19), channel_id=1, source_target_pairs={{0,12},{4,16},{8,21},{12,25},{16,30},{20,2},{24,7},{28,11}} | collective-permute-start | bytes 393224 | tf_op jit(solution)/shard_map/ppermute | solution.py:232
  15.2 10.7 %collective-permute-start.17 = (f32[64,512]{1,0:T(8,128)}, f32[64,512]{1,0:T(8,128)}, u32[]{:S(2)}, u32[]{:S(2)}) collective-permute-start(f32[64,512]{1,0:T(8,128)} %get-tuple-element.18), channel_id=1, source_target_pairs={{0,8},{4,12},{8,17},{12,21},{16,26},{20,30},{24,3},{28,7}} | collective-permute-start | bytes 393224 | tf_op jit(solution)/shard_map/ppermute | solution.py:232
  17.1 9.4 %collective-permute-start.18 = (f32[64,512]{1,0:T(8,128)}, f32[64,512]{1,0:T(8,128)}, u32[]{:S(2)}, u32[]{:S(2)}) collective-permute-start(f32[64,512]{1,0:T(8,128)} %get-tuple-element.17), channel_id=1, source_target_pairs={{0,4},{4,8},{8,13},{12,17},{16,22},{20,26},{24,31},{28,3}} | collective-permute-start | bytes 393224 | tf_op jit(solution)/shard_map/ppermute | solution.py:232
  19.1 7.4 %collective-permute-start.19 = (f32[64,512]{1,0:T(8,128)}, f32[64,512]{1,0:T(8,128)}, u32[]{:S(2)}, u32[]{:S(2)}) collective-permute-start(f32[64,512]{1,0:T(8,128)} %get-tuple-element.16), channel_id=1, source_target_pairs={{0,0},{4,4},{8,9},{12,13},{16,18},{20,22},{24,27},{28,31}} | collective-permute-start | bytes 393224 | tf_op jit(solution)/shard_map/ppermute | solution.py:232
  23.8 59.2 %collective-permute-start = (f32[512,512]{1,0:T(8,128)S(1)}, f32[512,512]{1,0:T(8,128)S(1)}, u32[]{:S(2)}, u32[]{:S(2)}) collective-permute-start(f32[512,512]{1,0:T(8,128)S(1)} %slice.18), channel_id=1, source_target_pairs={{0,2},{4,6},{8,10},{12,14},{16,18},{20,22},{24,26},{28,30}} | collective-permute-start | bytes 3145736 | tf_op jit(solution)/shard_map/ppermute | solution.py:191
  25.2 19.1 %collective-permute-start.7 = (f32[128,768]{1,0:T(8,128)S(1)}, f32[128,768]{1,0:T(8,128)S(1)}, u32[]{:S(2)}, u32[]{:S(2)}) collective-permute-start(f32[128,768]{1,0:T(8,128)S(1)} %pad_maximum_fusion), channel_id=1, source_target_pairs={{0,2}} | collective-permute-start | bytes 1179656 | tf_op jit(solution)/shard_map/ppermute | solution.py:191
  25.9 13.2 %collective-permute-start.2 = (f32[128,512]{1,0:T(8,128)}, f32[128,512]{1,0:T(8,128)S(1)}, u32[]{:S(2)}, u32[]{:S(2)}) collective-permute-start(f32[128,512]{1,0:T(8,128)} %slice.19), channel_id=1, source_target_pairs={{0,16}} | collective-permute-start | bytes 786440 | tf_op jit(solution)/shard_map/ppermute | solution.py:191
  28.6 10.5 %collective-permute-start.20 = (f32[2,1,64,512]{3,2,1,0:T(8,128)S(1)}, f32[2,1,64,512]{3,2,1,0:T(8,128)S(1)}, u32[]{:S(2)}, u32[]{:S(2)}) collective-permute-start(f32[2,1,64,512]{3,2,1,0:T(8,128)S(1)} %maximum_bitcast_fusion), channel_id=1, source_target_pairs={{0,4},{4,8},{8,12},{12,16},{16,20},{20,24},{24,28},{28,0},{1,5},{5... | collective-permute-start | bytes 786440 | tf_op jit(solution)/shard_map/ppermute | solution.py:242
  28.7 16.9 %collective-permute-start.21 = (f32[2,1,64,512]{3,2,1,0:T(8,128)S(1)}, f32[2,1,64,512]{3,2,1,0:T(8,128)S(1)}, u32[]{:S(2)}, u32[]{:S(2)}) collective-permute-start(f32[2,1,64,512]{3,2,1,0:T(8,128)S(1)} %maximum_bitcast_fusion), channel_id=1, source_target_pairs={{0,8},{4,12},{8,16},{12,20},{16,24},{20,28},{24,0},{28,4},{1,9},{5... | collective-permute-start | bytes 786440 | tf_op jit(solution)/shard_map/ppermute | solution.py:242
  39.1 28.2 %collective-permute-start.22 = (f32[2,1,64,512]{3,2,1,0:T(8,128)S(1)}, f32[2,1,64,512]{3,2,1,0:T(8,128)S(1)}, u32[]{:S(2)}, u32[]{:S(2)}) collective-permute-start(f32[2,1,64,512]{3,2,1,0:T(8,128)S(1)} %maximum_bitcast_fusion), channel_id=1, source_target_pairs={{0,12},{4,16},{8,20},{12,24},{16,28},{20,0},{24,4},{28,8},{1,13},{... | collective-permute-start | bytes 786440 | tf_op jit(solution)/shard_map/ppermute | solution.py:242
  39.1 30.3 %collective-permute-start.23 = (f32[2,1,64,512]{3,2,1,0:T(8,128)S(1)}, f32[2,1,64,512]{3,2,1,0:T(8,128)S(1)}, u32[]{:S(2)}, u32[]{:S(2)}) collective-permute-start(f32[2,1,64,512]{3,2,1,0:T(8,128)S(1)} %maximum_bitcast_fusion), channel_id=1, source_target_pairs={{0,16},{4,20},{8,24},{12,28},{16,0},{20,4},{24,8},{28,12},{1,17},{... | collective-permute-start | bytes 786440 | tf_op jit(solution)/shard_map/ppermute | solution.py:242
  44.2 23.8 %collective-permute-start.3 = (f32[128,512]{1,0:T(8,128)S(1)}, f32[128,512]{1,0:T(8,128)S(1)}, u32[]{:S(2)}, u32[]{:S(2)}) collective-permute-start(f32[128,512]{1,0:T(8,128)S(1)} %broadcast_select_fusion.6), channel_id=1, source_target_pairs={{0,8},{16,24}} | collective-permute-start | bytes 786440 | tf_op jit(solution)/shard_map/ppermute | solution.py:191
  45.6 22.5 %collective-permute-start.8 = (f32[128,768]{1,0:T(8,128)S(1)}, f32[128,768]{1,0:T(8,128)S(1)}, u32[]{:S(2)}, u32[]{:S(2)}) collective-permute-start(f32[128,768]{1,0:T(8,128)S(1)} %broadcast_select_fusion.1), channel_id=1, source_target_pairs={{0,4},{2,6}} | collective-permute-start | bytes 1179656 | tf_op jit(solution)/shard_map/ppermute | solution.py:191
  67.3 9.2 %collective-permute-start.24 = (f32[2,1,64,512]{3,2,1,0:T(8,128)S(1)}, f32[2,1,64,512]{3,2,1,0:T(8,128)S(1)}, u32[]{:S(2)}, u32[]{:S(2)}) collective-permute-start(f32[2,1,64,512]{3,2,1,0:T(8,128)S(1)} %maximum_bitcast_fusion), channel_id=1, source_target_pairs={{0,20},{4,24},{8,28},{12,0},{16,4},{20,8},{24,12},{28,16},{1,21},{... | collective-permute-start | bytes 786440 | tf_op jit(solution)/shard_map/ppermute | solution.py:242
  68.0 30.2 %collective-permute-start.25 = (f32[2,1,64,512]{3,2,1,0:T(8,128)S(1)}, f32[2,1,64,512]{3,2,1,0:T(8,128)S(1)}, u32[]{:S(2)}, u32[]{:S(2)}) collective-permute-start(f32[2,1,64,512]{3,2,1,0:T(8,128)S(1)} %maximum_bitcast_fusion), channel_id=1, source_target_pairs={{0,24},{4,28},{8,0},{12,4},{16,8},{20,12},{24,16},{28,20},{1,25},{... | collective-permute-start | bytes 786440 | tf_op jit(solution)/shard_map/ppermute | solution.py:242
  68.0 7.8 %collective-permute-start.4 = (f32[128,512]{1,0:T(8,128)S(1)}, f32[128,512]{1,0:T(8,128)S(1)}, u32[]{:S(2)}, u32[]{:S(2)}) collective-permute-start(f32[128,512]{1,0:T(8,128)S(1)} %broadcast_select_fusion.7), channel_id=1, source_target_pairs={{0,4},{16,20},{8,12},{24,28}} | collective-permute-start | bytes 786440 | tf_op jit(solution)/shard_map/ppermute | solution.py:191
  69.4 9.1 %collective-permute-start.9 = (f32[128,768]{1,0:T(8,128)S(1)}, f32[128,768]{1,0:T(8,128)S(1)}, u32[]{:S(2)}, u32[]{:S(2)}) collective-permute-start(f32[128,768]{1,0:T(8,128)S(1)} %broadcast_select_fusion.2), channel_id=1, source_target_pairs={{0,8},{2,10},{4,12},{6,14}} | collective-permute-start | bytes 1179656 | tf_op jit(solution)/shard_map/ppermute | solution.py:191
  75.8 23.1 %collective-permute-start.26 = (f32[2,1,64,512]{3,2,1,0:T(8,128)S(1)}, f32[2,1,64,512]{3,2,1,0:T(8,128)S(1)}, u32[]{:S(2)}, u32[]{:S(2)}) collective-permute-start(f32[2,1,64,512]{3,2,1,0:T(8,128)S(1)} %maximum_bitcast_fusion), channel_id=1, source_target_pairs={{0,28},{4,0},{8,4},{12,8},{16,12},{20,16},{24,20},{28,24},{1,29},{... | collective-permute-start | bytes 786440 | tf_op jit(solution)/shard_map/ppermute | solution.py:242
  76.5 5.2 %collective-permute-start.5 = (f32[128,512]{1,0:T(8,128)S(1)}, f32[128,512]{1,0:T(8,128)S(1)}, u32[]{:S(2)}, u32[]{:S(2)}) collective-permute-start(f32[128,512]{1,0:T(8,128)S(1)} %broadcast_select_fusion.8), channel_id=1, source_target_pairs={{0,2},{16,18},{8,10},{24,26},{4,6},{20,22},{12,14},{28,30}} | collective-permute-start | bytes 786440 | tf_op jit(solution)/shard_map/ppermute | solution.py:191
  78.5 18.3 %collective-permute-start.10 = (f32[128,768]{1,0:T(8,128)S(1)}, f32[128,768]{1,0:T(8,128)S(1)}, u32[]{:S(2)}, u32[]{:S(2)}) collective-permute-start(f32[128,768]{1,0:T(8,128)S(1)} %broadcast_select_fusion.3), channel_id=1, source_target_pairs={{0,16},{2,18},{4,20},{6,22},{8,24},{10,26},{12,28},{14,30}} | collective-permute-start | bytes 1179656 | tf_op jit(solution)/shard_map/ppermute | solution.py:191
  81.7 18.0 %collective-permute-start.6 = (f32[128,512]{1,0:T(8,128)S(1)}, f32[128,512]{1,0:T(8,128)S(1)}, u32[]{:S(2)}, u32[]{:S(2)}) collective-permute-start(f32[128,512]{1,0:T(8,128)S(1)} %broadcast_select_fusion.9), channel_id=1, source_target_pairs={{0,1},{16,17},{8,9},{24,25},{4,5},{20,21},{12,13},{28,29},{2,3},{1... | collective-permute-start | bytes 786440 | tf_op jit(solution)/shard_map/ppermute | solution.py:191
  83.2 57.2 %collective-permute-start.1 = (f32[512,512]{1,0:T(8,128)S(1)}, f32[512,512]{1,0:T(8,128)S(1)}, u32[]{:S(2)}, u32[]{:S(2)}) collective-permute-start(f32[512,512]{1,0:T(8,128)S(1)} %broadcast_select_fusion), channel_id=1, source_target_pairs={{0,1},{2,3},{4,5},{6,7},{8,9},{10,11},{12,13},{14,15},{16,17},{18,... | collective-permute-start | bytes 3145736 | tf_op jit(solution)/shard_map/ppermute | solution.py:191
  96.9 12.3 %collective-permute-start.11 = (f32[128,768]{1,0:T(8,128)S(1)}, f32[128,768]{1,0:T(8,128)S(1)}, u32[]{:S(2)}, u32[]{:S(2)}) collective-permute-start(f32[128,768]{1,0:T(8,128)S(1)} %broadcast_select_fusion.4), channel_id=1, source_target_pairs={{0,1},{2,3},{4,5},{6,7},{8,9},{10,11},{12,13},{14,15},{16,17},{18,... | collective-permute-start | bytes 1179656 | tf_op jit(solution)/shard_map/ppermute | solution.py:191
  136.6 3.8 %copy-start.2 = (f32[512,512]{1,0:T(8,128)S(1)}, f32[512,512]{1,0:T(8,128)}, u32[]{:S(2)}) copy-start(f32[512,512]{1,0:T(8,128)} %get-tuple-element.10) | copy-start | bytes 3145732
  140.4 1.6 %copy-start.1 = (f32[512,1024]{0,1:T(8,128)S(1)}, f32[512,1024]{0,1:T(8,128)}, u32[]{:S(2)}) copy-start(f32[512,1024]{0,1:T(8,128)} %copy.6) | copy-start | bytes 6291460

commit v2 on v1

--- a/solution.py
+++ b/solution.py
@@ -183,15 +183,13 @@
     )(top, inv, log, rest)
 
 
-def tree_rounds(value, axes, strides):
+def tree_rounds(value, axes, strides, have=(0,)):
     index = lax.axis_index(axes)
-    size = lax.axis_size(axes)
-    have = [0]
+    have = list(have)
     for stride in strides:
         got = lax.ppermute(value, axes, [(s, s + stride) for s in have])
         value = jnp.where((index // stride) % 2 == 1, got, value)
         have = have + [s + stride for s in have]
-    assert len(have) == size
     return value
 
 
@@ -217,33 +215,50 @@
         [block[k * LANES : (k + 1) * LANES, k * LANES : width] for k in range(1, count)], axis=1
     )
     row_strides, col_strides = halvings(rows_n, cols_n), halvings(cols_n)
-    first = tree_rounds(first, both, row_strides + col_strides)
+    first = tree_rounds(first, both, row_strides)
     rest = tree_rounds(rest, both, col_strides[:-1] + row_strides[::-1] + col_strides[-1:])
-
-    held = block[:, :width]
-    piece_rows = width // rows_n
-    pieces = held.reshape(rows_n, piece_rows, width)
-    slots = [jnp.zeros((piece_rows, width), jnp.float32) for _ in range(per_col)]
-    for s in range(rows_n):
-        mine = lax.dynamic_index_in_dim(pieces, (row + s) % rows_n, 0, keepdims=False)
-        pairs = [
-            (r * cols_n, ((r + s) % rows_n) * cols_n + r // per_col) for r in range(rows_n)
+    own = tree_rounds(block[:, :width], "col", col_strides[:-1])
+    first, own = lax.optimization_barrier((first, own))
+    own = tree_rounds(own, "col", col_strides[-1:], range(0, cols_n, 2))
+    first = tree_rounds(first, both, col_strides, range(0, rows_n * cols_n, cols_n))
+
+    far = own
+    low, size = 0, 1
+    while size < cols_n:
+        moves = [
+            (low + i, low - 1 - i if i < size // 2 else low + 2 * size - 1 - i) for i in range(size)
         ]
-        got = lax.ppermute(mine, both, pairs)
-        slots = [
-            jnp.where((row - per_col * col - b) % rows_n == s, got, slots[b]) for b in range(per_col)
-        ]
-    piece = jnp.stack(slots)[:, None]
-    own = tree_rounds(held, "col", col_strides)
-
-    far = jnp.zeros((per_col, rows_n, piece_rows, width), jnp.float32)
-    far = lax.dynamic_update_slice(far, piece, (0, row, 0, 0))
-    for s in range(1, rows_n):
-        got = lax.ppermute(piece, "row", [(i, (i + s) % rows_n) for i in range(rows_n)])
-        far = lax.dynamic_update_slice(far, got, (0, (row - s) % rows_n, 0, 0))
-    far = far.reshape(cols, width)
+        if 2 * size == cols_n:
+            first, far = lax.optimization_barrier((first, far))
+        got = lax.ppermute(
+            far,
+            both,
+            [
+                (
+                    (((c + src) % cols_n) * per_col + b) * cols_n + c,
+                    (((c + dst) % cols_n) * per_col + b) * cols_n + c,
+                )
+                for c in range(cols_n)
+                for b in range(per_col)
+                for src, dst in moves
+            ],
+        )
+        offset = (row // per_col - col) % cols_n
+        takes = jnp.zeros((), bool)
+        for _, dst in moves:
+            takes = takes | (offset == dst % cols_n)
+        far = jnp.where(takes, got, far)
+        low, size = low - size // 2, 2 * size
 
     top, inv, log = first_panel(first, count)
+    top, far = lax.optimization_barrier((top, far))
+    parts = jnp.zeros((per_col, width, width), jnp.float32)
+    parts = lax.dynamic_update_slice(parts, far[None], (row % per_col, 0, 0))
+    for s in range(1, per_col):
+        pairs = [(r, r - r % per_col + (r % per_col + s) % per_col) for r in range(rows_n)]
+        got = lax.ppermute(far, "row", pairs)
+        parts = lax.dynamic_update_slice(parts, got[None], ((row - s) % per_col, 0, 0))
+    far = parts.reshape(cols, width)
     inverse, log = other_panels(top, inv, log, rest, count)
 
     high = lax.Precision.HIGH

time: 146 us -> 143 us (0.979)
  starting transfers between devices: 44.2 us -> 27.6 us
  waiting for transfers between devices: 39.4 us -> 51.1 us
  other arithmetic: 4.88 us -> 13.3 us
  local copies, waits for them, and re-layouts: 15 us -> 10.2 us
  matrix products: 6.86 us -> 4.91 us
    ppermute x12, waiting for transfers between devices: 19.1 us -> 51 us  [tree_rounds(): got = lax.ppermute(value, axes, [(s, s + stride) for s in have])]
    ppermute x15 -> x3, starting transfers between devices: 30.9 us -> 5.95 us  [the longest x1 3.01 us: per_device(): got = lax.ppermute(far, 'row', pairs)]
    ppermute x15 -> x3, waiting for transfers between devices: 20.4 us -> 0.01 us  [the longest x2 0.01 us: per_device(): lax.ppermute(far, both, [(((c + src) % cols_n * per_col + b) * cols_n + c...]
    ppermute x12, starting transfers between devices: 13.3 us -> 21.7 us  [tree_rounds(): got = lax.ppermute(value, axes, [(s, s + stride) for s in have])]
    select_n x11 -> x12, other arithmetic: 2.06 us -> 8.9 us  [tree_rounds(): value = jnp.where(index // stride % 2 == 1, got, value)]
    select_n x0 -> x2, other arithmetic: none -> 3.61 us  [per_device(): far = jnp.where(takes, got, far)]
    dynamic_update_slice x7 -> x2, local copies, waits for them, and re-layouts: 5.05 us -> 2.65 us  [the longest x1 1.35 us: per_device(): parts = lax.dynamic_update_slice(parts, far[None], (row % per_col, 0, 0))]
    another operation x2 -> x0, other arithmetic: 2.04 us -> none  [per_device(): piece = jnp.stack(slots)[:, None]]
  transfers between devices with their start and end apart: 27 -> 15, of which waited for: 5 -> 3; matrix products, arithmetic and copies ran while one was open for 13% -> 14% of each run, Pallas kernels for 23% -> 24%
where the time goes in v2:
time: 143 us; the launch traced here: 142 us
  waiting for transfers between devices  51.1 us (36%)
  Pallas kernels  34.1 us (24%)
  starting transfers between devices  27.6 us (19%)
  other arithmetic  13.3 us (9%)
  local copies, waits for them, and re-layouts  10.2 us (7%)
  matrix products  4.91 us (3%)
    ppermute x12, waiting for transfers between devices, tree_rounds(): got = lax.ppermute(value, axes, [(s, s + stride) for s in have])  51 us
    pallas_call x1, Pallas kernels, other_panels(): pl.pallas_call(body, out_shape=[jax.ShapeDtypeStruct((count * LANES, coun...  25.3 us
    ppermute x12, starting transfers between devices, tree_rounds(): got = lax.ppermute(value, axes, [(s, s + stride) for s in have])  21.7 us
    select_n x12, other arithmetic, tree_rounds(): value = jnp.where(index // stride % 2 == 1, got, value)  8.9 us
    pallas_call x1, Pallas kernels, first_panel(): pl.pallas_call(body, out_shape=[jax.ShapeDtypeStruct((LANES, count * LANE...  8.75 us
    unnamed x16, local copies, waits for them, and re-layouts  3.66 us
    select_n x2, other arithmetic, per_device(): far = jnp.where(takes, got, far)  3.61 us
    ppermute x1, starting transfers between devices, per_device(): got = lax.ppermute(far, 'row', pairs)  3.01 us
  transfers between devices with their start and end apart: 15, of which 3 were waited for; matrix products, arithmetic and copies ran while one was open for 14% of the time, Pallas kernels for 24%

profile of v2, /device:TPU:24, one launch (start us, length us, event | category | flops | bytes accessed | tf_op | source)
XLA Modules:
  0.0 142.1 jit_solution(17097286168984971125)
XLA Ops:
  0.6 1.1 slice.18
  1.8 1.4 collective-permute-start
  3.1 1.3 slice.19
  4.4 4.4 %collective-permute-start.3 = (f32[512,512]{1,0:T(8,128)S(1)}, f32[512,512]{1,0:T(8,128)}, u32[]{:S(2)}, u32[]{:S(2)}) collective-permute-start(f32[512,512]{1,0:T(8,128)S(1)} %slice.19), channel_id=1, source_target_pairs={{0,2},{4,6},{8,10},{12,14},{16,18},{20,22},{24,26},{28,30}} | collective-permute-start | bytes 3145736 | tf_op jit(solution)/shard_map/ppermute | solution.py:190
  9.9 1.3 collective-permute-start.1
  11.2 7.0 %collective-permute-done.1 = f32[128,512]{1,0:T(8,128)} collective-permute-done((f32[128,512]{1,0:T(8,128)S(1)}, f32[128,512]{1,0:T(8,128)}, u32[]{:S(2)}, u32[]{:S(2)}) %collective-permute-start.1) | collective-permute-done | bytes 262176 | tf_op jit(solution)/shard_map/ppermute | solution.py:190
  19.2 2.0 %collective-permute-start.2 = (f32[128,512]{1,0:T(8,128)S(1)}, f32[128,512]{1,0:T(8,128)}, u32[]{:S(2)}, u32[]{:S(2)}) collective-permute-start(f32[128,512]{1,0:T(8,128)S(1)} %broadcast_select_fusion.12), channel_id=1, source_target_pairs={{0,4},{16,20},{8,12},{24,28}} | collective-permute-start | bytes 786440 | tf_op jit(solution)/shard_map/ppermute | solution.py:190
  21.2 3.2 %collective-permute-done.2 = f32[128,512]{1,0:T(8,128)} collective-permute-done((f32[128,512]{1,0:T(8,128)S(1)}, f32[128,512]{1,0:T(8,128)}, u32[]{:S(2)}, u32[]{:S(2)}) %collective-permute-start.2) | collective-permute-done | bytes 262176 | tf_op jit(solution)/shard_map/ppermute | solution.py:190
  25.4 2.3 %collective-permute-start.4 = (f32[512,512]{1,0:T(8,128)S(1)}, f32[512,512]{1,0:T(8,128)}, u32[]{:S(2)}, u32[]{:S(2)}) collective-permute-start(f32[512,512]{1,0:T(8,128)S(1)} %broadcast_select_fusion.2), channel_id=1, source_target_pairs={{0,1},{2,3},{4,5},{6,7},{8,9},{10,11},{12,13},{14,15},{16,17},{18,... | collective-permute-start | bytes 3145736 | tf_op jit(solution)/shard_map/ppermute | solution.py:190
  28.5 1.4 collective-permute-start.9
  29.9 1.4 %collective-permute-start.5 = (f32[128,512]{1,0:T(8,128)}, f32[128,512]{1,0:T(8,128)S(1)}, u32[]{:S(2)}, u32[]{:S(2)}) collective-permute-start(f32[128,512]{1,0:T(8,128)} %broadcast_select_fusion.13), channel_id=1, source_target_pairs={{0,2},{4,6},{8,10},{12,14},{16,18},{20,22},{24,26},{28,30}} | collective-permute-start | bytes 786440 | tf_op jit(solution)/shard_map/ppermute | solution.py:190
  31.4 1.4 %broadcast_select_fusion.3 = f32[512,512]{1,0:T(8,128)S(1)} fusion(f32[512,512]{1,0:T(8,128)} %collective-permute-done.4, f32[512,512]{1,0:T(8,128)} %copy-done.3, pred[]{:T(512)S(6)} %eq.61), kind=kLoop, calls=%fused_computation.9 | loop fusion | flops 262144 | bytes 3145729 | tf_op jit(solution)/shard_map/jit(_where)/select_n | solution.py:191
  32.8 1.7 %collective-permute-start.7 = (f32[512,512]{1,0:T(8,128)S(1)}, f32[512,512]{1,0:T(8,128)}, u32[]{:S(2)}, u32[]{:S(2)}) collective-permute-start(f32[512,512]{1,0:T(8,128)S(1)} %broadcast_select_fusion.3), channel_id=1, source_target_pairs={{0,8},{4,12},{9,17},{13,21},{18,26},{22,30},{27,3},{31,7}} | collective-permute-start | bytes 3145736 | tf_op jit(solution)/shard_map/ppermute | solution.py:233
  35.3 1.4 collective-permute-start.10
  36.7 2.0 %collective-permute-start.6 = (f32[128,512]{1,0:T(8,128)S(1)}, f32[128,512]{1,0:T(8,128)}, u32[]{:S(2)}, u32[]{:S(2)}) collective-permute-start(f32[128,512]{1,0:T(8,128)S(1)} %broadcast_select_fusion.9), channel_id=1, source_target_pairs={{0,1},{4,5},{8,9},{12,13},{16,17},{20,21},{24,25},{28,29},{2,3},{6... | collective-permute-start | bytes 786440 | tf_op jit(solution)/shard_map/ppermute | solution.py:190
  41.3 1.2 broadcast_select_fusion.1
  42.5 1.3 collective-permute-start.8
  43.8 1.3 collective-permute-start.12
  45.1 40.8 %collective-permute-done.12 = f32[128,768]{1,0:T(8,128)} collective-permute-done((f32[128,768]{1,0:T(8,128)S(1)}, f32[128,768]{1,0:T(8,128)}, u32[]{:S(2)}, u32[]{:S(2)}) %collective-permute-start.12) | collective-permute-done | bytes 393248 | tf_op jit(solution)/shard_map/ppermute | solution.py:190
  87.0 2.1 %collective-permute-start.13 = (f32[128,768]{1,0:T(8,128)S(1)}, f32[128,768]{1,0:T(8,128)}, u32[]{:S(2)}, u32[]{:S(2)}) collective-permute-start(f32[128,768]{1,0:T(8,128)S(1)} %broadcast_select_fusion.7), channel_id=1, source_target_pairs={{0,1},{2,3},{4,5},{6,7},{8,9},{10,11},{12,13},{14,15},{16,17},{18,... | collective-permute-start | bytes 1179656 | tf_op jit(solution)/shard_map/ppermute | solution.py:190
  89.1 8.7 %first_panel.1 = (f32[128,512]{1,0:T(8,128)}, f32[128,128]{1,0:T(8,128)}, f32[8,128]{1,0:T(8,128)}) custom-call(f32[128,512]{1,0:T(8,128)} %broadcast_select_fusion.10.top_ref), custom_call_target="tpu_custom_call" | custom-call | tf_op jit(solution)/shard_map/first_panel/pallas_call | solution.py:125
  97.8 2.4 %broadcast_select_fusion = f32[512,512]{1,0:T(8,128)} fusion(f32[512,512]{1,0:T(8,128)} %collective-permute-done.8, f32[512,512]{1,0:T(8,128)} %broadcast_select_fusion.1, pred[]{:T(512)S(6)} %or.11), kind=kLoop, calls=%fused_computation.6 | loop fusion | flops 262144 | bytes 3145729 | tf_op jit(solution)/shard_map/jit(_where)/select_n | solution.py:250
  100.2 3.0 %collective-permute-start.14 = (f32[512,512]{1,0:T(8,128)}, f32[512,512]{1,0:T(8,128)}, u32[]{:S(2)}, u32[]{:S(2)}) collective-permute-start(f32[512,512]{1,0:T(8,128)} %broadcast_select_fusion), channel_id=1, source_target_pairs={{0,4},{4,0},{8,12},{12,8},{16,20},{20,16},{24,28},{28,24},{1,5},{5... | collective-permute-start | bytes 3145736 | tf_op jit(solution)/shard_map/ppermute | solution.py:259
  103.2 1.8 %copy.3 = f32[512,1024]{0,1:T(8,128)} copy(f32[512,1024]{1,0:T(8,128)S(1)} %copy-done) | data formatting | bytes 4194304 | tf_op args[0]
  105.9 25.3 %other_panels.1 = (f32[512,512]{1,0:T(8,128)}, f32[8,128]{1,0:T(8,128)}) custom-call(f32[128,512]{1,0:T(8,128)} %get-tuple-element.18.top_ref, f32[128,128]{1,0:T(8,128)} %get-tuple-element.19.inv_ref, f32[8,128]{1,0:T(8,128)} %get-tuple-element.20.log_ref, f32[128,768]{1,0:T(8,128)} %broadcast_select_fusion.8.rest_ref), custom_call_target="tpu_custom_call" | custom-call | tf_op jit(solution)/shard_map/other_panels/pallas_call | solution.py:172
  131.2 1.2 slice.23
  132.6 1.4 bitcast_dynamic-update-slice_fusion.1
  134.0 1.1 fusion.1
  135.1 1.3 bitcast_dynamic-update-slice_fusion
  136.4 1.9 %fusion.7 = f32[1024,512]{1,0:T(8,128)S(1)} fusion(f32[1024,512]{1,0:T(8,128)S(1)} %bitcast.12, f32[512,512]{1,0:T(8,128)S(1)} %copy-done.2), kind=kOutput, calls=%fused_computation.30 | convolution fusion | flops 1610612736 | bytes 5242880 | tf_op jit(solution)/shard_map/dot_general | solution.py:267
  138.3 2.0 %maximum_select_fusion = f32[512,1024]{0,1:T(8,128)S(1)} fusion(f32[512,512]{0,1:T(8,128)S(1)} %get-tuple-element.26, f32[512,1024]{0,1:T(8,128)S(1)} %copy-done.1, f32[512,512]{0,1:T(8,128)S(1)} %get-tuple-element.27, f32[1024,512]{1,0:T(8,128)S(1)} %fusion.7, pred[1024]{0:T(1024)(128)(4,1)S(1)} %fusion.3, pred[]{:T(512)S(6)} %gt.4), kind=kOutput, calls=%fused_computation | convolution fusion | flops 1612709888 | bytes 8389633 | tf_op jit(solution)/shard_map/dot_general | solution.py:268
  140.2 1.8 %copy.5 = f32[512,1024]{1,0:T(8,128)} copy(f32[512,1024]{0,1:T(8,128)S(1)} %maximum_select_fusion) | data formatting | bytes 4194304
  (44 shorter events, 9.3 us)
Async XLA Ops:
  0.6 8.2 %copy-start = (f32[512,1024]{1,0:T(8,128)S(1)}, f32[512,1024]{1,0:T(8,128)}, u32[]{:S(2)}) copy-start(f32[512,1024]{1,0:T(8,128)} %param.1) | copy-start | bytes 6291460
  1.8 7.1 %collective-permute-start = (f32[128,512]{1,0:T(8,128)S(1)}, f32[128,512]{1,0:T(8,128)}, u32[]{:S(2)}, u32[]{:S(2)}) collective-permute-start(f32[128,512]{1,0:T(8,128)S(1)} %slice.18), channel_id=1, source_target_pairs={{0,16}} | collective-permute-start | bytes 786440 | tf_op jit(solution)/shard_map/ppermute | solution.py:190
  4.4 20.7 %collective-permute-start.3 = (f32[512,512]{1,0:T(8,128)S(1)}, f32[512,512]{1,0:T(8,128)}, u32[]{:S(2)}, u32[]{:S(2)}) collective-permute-start(f32[512,512]{1,0:T(8,128)S(1)} %slice.19), channel_id=1, source_target_pairs={{0,2},{4,6},{8,10},{12,14},{16,18},{20,22},{24,26},{28,30}} | collective-permute-start | bytes 3145736 | tf_op jit(solution)/shard_map/ppermute | solution.py:190
  9.8 1.3 copy-start.6
  9.9 8.4 %collective-permute-start.1 = (f32[128,512]{1,0:T(8,128)S(1)}, f32[128,512]{1,0:T(8,128)}, u32[]{:S(2)}, u32[]{:S(2)}) collective-permute-start(f32[128,512]{1,0:T(8,128)S(1)} %broadcast_select_fusion.11), channel_id=1, source_target_pairs={{0,8},{16,24}} | collective-permute-start | bytes 786440 | tf_op jit(solution)/shard_map/ppermute | solution.py:190
  19.2 5.2 %collective-permute-start.2 = (f32[128,512]{1,0:T(8,128)S(1)}, f32[128,512]{1,0:T(8,128)}, u32[]{:S(2)}, u32[]{:S(2)}) collective-permute-start(f32[128,512]{1,0:T(8,128)S(1)} %broadcast_select_fusion.12), channel_id=1, source_target_pairs={{0,4},{16,20},{8,12},{24,28}} | collective-permute-start | bytes 786440 | tf_op jit(solution)/shard_map/ppermute | solution.py:190
  25.4 6.0 %copy-start.3 = (f32[512,512]{1,0:T(8,128)}, f32[512,512]{1,0:T(8,128)S(1)}, u32[]{:S(2)}) copy-start(f32[512,512]{1,0:T(8,128)S(1)} %broadcast_select_fusion.2) | copy-start | bytes 3145732
  25.4 6.0 %collective-permute-start.4 = (f32[512,512]{1,0:T(8,128)S(1)}, f32[512,512]{1,0:T(8,128)}, u32[]{:S(2)}, u32[]{:S(2)}) collective-permute-start(f32[512,512]{1,0:T(8,128)S(1)} %broadcast_select_fusion.2), channel_id=1, source_target_pairs={{0,1},{2,3},{4,5},{6,7},{8,9},{10,11},{12,13},{14,15},{16,17},{18,... | collective-permute-start | bytes 3145736 | tf_op jit(solution)/shard_map/ppermute | solution.py:190
  28.5 6.0 %collective-permute-start.9 = (f32[128,768]{1,0:T(8,128)}, f32[128,768]{1,0:T(8,128)}, u32[]{:S(2)}, u32[]{:S(2)}) collective-permute-start(f32[128,768]{1,0:T(8,128)} %pad_maximum_fusion), channel_id=1, source_target_pairs={{0,2}} | collective-permute-start | bytes 1179656 | tf_op jit(solution)/shard_map/ppermute | solution.py:190
  29.9 6.8 %copy-start.5 = (f32[128,512]{1,0:T(8,128)S(1)}, f32[128,512]{1,0:T(8,128)}, u32[]{:S(2)}) copy-start(f32[128,512]{1,0:T(8,128)} %broadcast_select_fusion.13) | copy-start | bytes 786436
  29.9 6.8 %collective-permute-start.5 = (f32[128,512]{1,0:T(8,128)}, f32[128,512]{1,0:T(8,128)S(1)}, u32[]{:S(2)}, u32[]{:S(2)}) collective-permute-start(f32[128,512]{1,0:T(8,128)} %broadcast_select_fusion.13), channel_id=1, source_target_pairs={{0,2},{4,6},{8,10},{12,14},{16,18},{20,22},{24,26},{28,30}} | collective-permute-start | bytes 786440 | tf_op jit(solution)/shard_map/ppermute | solution.py:190
  32.8 8.5 %collective-permute-start.7 = (f32[512,512]{1,0:T(8,128)S(1)}, f32[512,512]{1,0:T(8,128)}, u32[]{:S(2)}, u32[]{:S(2)}) collective-permute-start(f32[512,512]{1,0:T(8,128)S(1)} %broadcast_select_fusion.3), channel_id=1, source_target_pairs={{0,8},{4,12},{9,17},{13,21},{18,26},{22,30},{27,3},{31,7}} | collective-permute-start | bytes 3145736 | tf_op jit(solution)/shard_map/ppermute | solution.py:233
  35.3 3.5 %collective-permute-start.10 = (f32[128,768]{1,0:T(8,128)}, f32[128,768]{1,0:T(8,128)}, u32[]{:S(2)}, u32[]{:S(2)}) collective-permute-start(f32[128,768]{1,0:T(8,128)} %broadcast_select_fusion.4), channel_id=1, source_target_pairs={{0,4},{2,6}} | collective-permute-start | bytes 1179656 | tf_op jit(solution)/shard_map/ppermute | solution.py:190
  36.7 3.7 %collective-permute-start.6 = (f32[128,512]{1,0:T(8,128)S(1)}, f32[128,512]{1,0:T(8,128)}, u32[]{:S(2)}, u32[]{:S(2)}) collective-permute-start(f32[128,512]{1,0:T(8,128)S(1)} %broadcast_select_fusion.9), channel_id=1, source_target_pairs={{0,1},{4,5},{8,9},{12,13},{16,17},{20,21},{24,25},{28,29},{2,3},{6... | collective-permute-start | bytes 786440 | tf_op jit(solution)/shard_map/ppermute | solution.py:190
  39.8 4.0 %collective-permute-start.11 = (f32[128,768]{1,0:T(8,128)S(1)}, f32[128,768]{1,0:T(8,128)S(1)}, u32[]{:S(2)}, u32[]{:S(2)}) collective-permute-start(f32[128,768]{1,0:T(8,128)S(1)} %broadcast_select_fusion.5), channel_id=1, source_target_pairs={{0,8},{2,10},{4,12},{6,14}} | collective-permute-start | bytes 1179656 | tf_op jit(solution)/shard_map/ppermute | solution.py:190
  42.5 55.3 %collective-permute-start.8 = (f32[512,512]{1,0:T(8,128)}, f32[512,512]{1,0:T(8,128)}, u32[]{:S(2)}, u32[]{:S(2)}) collective-permute-start(f32[512,512]{1,0:T(8,128)} %broadcast_select_fusion.1), channel_id=1, source_target_pairs={{0,24},{8,16},{4,28},{12,20},{9,1},{17,25},{13,5},{21,29},{18,10},... | collective-permute-start | bytes 3145736 | tf_op jit(solution)/shard_map/ppermute | solution.py:233
  43.8 1.3 copy-start.4
  43.8 42.1 %collective-permute-start.12 = (f32[128,768]{1,0:T(8,128)S(1)}, f32[128,768]{1,0:T(8,128)}, u32[]{:S(2)}, u32[]{:S(2)}) collective-permute-start(f32[128,768]{1,0:T(8,128)S(1)} %broadcast_select_fusion.6), channel_id=1, source_target_pairs={{0,16},{2,18},{4,20},{6,22},{8,24},{10,26},{12,28},{14,30}} | collective-permute-start | bytes 1179656 | tf_op jit(solution)/shard_map/ppermute | solution.py:190
  87.0 18.1 %collective-permute-start.13 = (f32[128,768]{1,0:T(8,128)S(1)}, f32[128,768]{1,0:T(8,128)}, u32[]{:S(2)}, u32[]{:S(2)}) collective-permute-start(f32[128,768]{1,0:T(8,128)S(1)} %broadcast_select_fusion.7), channel_id=1, source_target_pairs={{0,1},{2,3},{4,5},{6,7},{8,9},{10,11},{12,13},{14,15},{16,17},{18,... | collective-permute-start | bytes 1179656 | tf_op jit(solution)/shard_map/ppermute | solution.py:190
  100.2 34.8 %collective-permute-start.14 = (f32[512,512]{1,0:T(8,128)}, f32[512,512]{1,0:T(8,128)}, u32[]{:S(2)}, u32[]{:S(2)}) collective-permute-start(f32[512,512]{1,0:T(8,128)} %broadcast_select_fusion), channel_id=1, source_target_pairs={{0,4},{4,0},{8,12},{12,8},{16,20},{20,16},{24,28},{28,24},{1,5},{5... | collective-permute-start | bytes 3145736 | tf_op jit(solution)/shard_map/ppermute | solution.py:259
  132.4 1.6 %copy-start.2 = (f32[512,512]{1,0:T(8,128)S(1)}, f32[512,512]{1,0:T(8,128)}, u32[]{:S(2)}) copy-start(f32[512,512]{1,0:T(8,128)} %get-tuple-element.21) | copy-start | bytes 3145732
  136.4 1.9 %copy-start.1 = (f32[512,1024]{0,1:T(8,128)S(1)}, f32[512,1024]{0,1:T(8,128)}, u32[]{:S(2)}) copy-start(f32[512,1024]{0,1:T(8,128)} %copy.3) | copy-start | bytes 6291460

commit v3 on v2

--- a/solution.py
+++ b/solution.py
@@ -193,6 +193,13 @@
     return value
 
 
+def reach(strides):
+    have = [0]
+    for stride in strides:
+        have = have + [s + stride for s in have]
+    return have
+
+
 def halvings(size, unit=1):
     out = []
     while size > 1:
@@ -215,12 +222,14 @@
         [block[k * LANES : (k + 1) * LANES, k * LANES : width] for k in range(1, count)], axis=1
     )
     row_strides, col_strides = halvings(rows_n, cols_n), halvings(cols_n)
+    order = row_strides[-1:] + row_strides[:-1] + col_strides
     first = tree_rounds(first, both, row_strides)
-    rest = tree_rounds(rest, both, col_strides[:-1] + row_strides[::-1] + col_strides[-1:])
+    rest = tree_rounds(rest, both, order[:1])
     own = tree_rounds(block[:, :width], "col", col_strides[:-1])
-    first, own = lax.optimization_barrier((first, own))
+    first, rest, own = lax.optimization_barrier((first, rest, own))
     own = tree_rounds(own, "col", col_strides[-1:], range(0, cols_n, 2))
     first = tree_rounds(first, both, col_strides, range(0, rows_n * cols_n, cols_n))
+    rest = tree_rounds(rest, both, order[1:-2], reach(order[:1]))
 
     far = own
     low, size = 0, 1
@@ -229,7 +238,7 @@
             (low + i, low - 1 - i if i < size // 2 else low + 2 * size - 1 - i) for i in range(size)
         ]
         if 2 * size == cols_n:
-            first, far = lax.optimization_barrier((first, far))
+            first, rest, far = lax.optimization_barrier((first, rest, far))
         got = lax.ppermute(
             far,
             both,
@@ -250,8 +259,10 @@
         far = jnp.where(takes, got, far)
         low, size = low - size // 2, 2 * size
 
+    rest = tree_rounds(rest, both, order[-2:-1], reach(order[:-2]))
     top, inv, log = first_panel(first, count)
-    top, far = lax.optimization_barrier((top, far))
+    top, rest, far = lax.optimization_barrier((top, rest, far))
+    rest = tree_rounds(rest, both, order[-1:], reach(order[:-1]))
     parts = jnp.zeros((per_col, width, width), jnp.float32)
     parts = lax.dynamic_update_slice(parts, far[None], (row % per_col, 0, 0))
     for s in range(1, per_col):

time: 143 us -> 127 us (0.89)
  the two profiles are of different devices: /device:TPU:24 before, /device:TPU:16 now
where the time goes in v3:
time: 127 us; the launch traced here: 126 us
  Pallas kernels  34 us (27%)
  starting transfers between devices  32.7 us (26%)
  waiting for transfers between devices  29 us (23%)
  other arithmetic  12.3 us (10%)
  local copies, waits for them, and re-layouts  11.3 us (9%)
  matrix products  6.09 us (5%)
    ppermute x12, starting transfers between devices, tree_rounds(): got = lax.ppermute(value, axes, [(s, s + stride) for s in have])  27.9 us
    pallas_call x1, Pallas kernels, other_panels(): pl.pallas_call(body, out_shape=[jax.ShapeDtypeStruct((count * LANES, coun...  25.3 us
    ppermute x2, waiting for transfers between devices, per_device(): lax.ppermute(far, both, [(((c + src) % cols_n * per_col + b) * cols_n + c...  17.6 us
    ppermute x12, waiting for transfers between devices, tree_rounds(): got = lax.ppermute(value, axes, [(s, s + stride) for s in have])  11.3 us
    pallas_call x1, Pallas kernels, first_panel(): pl.pallas_call(body, out_shape=[jax.ShapeDtypeStruct((LANES, count * LANE...  8.75 us
    select_n x12, other arithmetic, tree_rounds(): value = jnp.where(index // stride % 2 == 1, got, value)  8.64 us
    unnamed x14, local copies, waits for them, and re-layouts  3.78 us
    select_n x2, other arithmetic, per_device(): far = jnp.where(takes, got, far)  3.62 us
  transfers between devices with their start and end apart: 15, of which 6 were waited for; matrix products, arithmetic and copies ran while one was open for 14% of the time, Pallas kernels for 27%

profile of v3, /device:TPU:16, one launch (start us, length us, event | category | flops | bytes accessed | tf_op | source)
XLA Modules:
  0.0 126.3 jit_solution(9842790091115362848)
XLA Ops:
  1.8 1.3 %collective-permute-start = (f32[128,512]{1,0:T(8,128)S(1)}, f32[128,512]{1,0:T(8,128)S(1)}, u32[]{:S(2)}, u32[]{:S(2)}) collective-permute-start(f32[128,512]{1,0:T(8,128)S(1)} %slice.18), channel_id=1, source_target_pairs={{0,16}} | collective-permute-start | bytes 786440 | tf_op jit(solution)/shard_map/ppermute | solution.py:190
  3.1 2.3 %slice.22 = f32[512,512]{1,0:T(8,128)} slice(f32[512,1024]{1,0:T(8,128)} %param.1), slice={[0:512], [0:512]} | slice | bytes 2097152 | tf_op jit(solution)/shard_map/slice | solution.py:228
  5.3 3.8 %collective-permute-start.4 = (f32[512,512]{1,0:T(8,128)}, f32[512,512]{1,0:T(8,128)}, u32[]{:S(2)}, u32[]{:S(2)}) collective-permute-start(f32[512,512]{1,0:T(8,128)} %slice.22), channel_id=1, source_target_pairs={{0,2},{4,6},{8,10},{12,14},{16,18},{20,22},{24,26},{28,30}} | collective-permute-start | bytes 3145736 | tf_op jit(solution)/shard_map/ppermute | solution.py:190
  9.1 1.8 %collective-permute-done = f32[128,512]{1,0:T(8,128)S(1)} collective-permute-done((f32[128,512]{1,0:T(8,128)S(1)}, f32[128,512]{1,0:T(8,128)S(1)}, u32[]{:S(2)}, u32[]{:S(2)}) %collective-permute-start) | collective-permute-done | bytes 262176 | tf_op jit(solution)/shard_map/ppermute | solution.py:190
  11.0 2.4 %collective-permute-start.1 = (f32[128,512]{1,0:T(8,128)S(1)}, f32[128,512]{1,0:T(8,128)}, u32[]{:S(2)}, u32[]{:S(2)}) collective-permute-start(f32[128,512]{1,0:T(8,128)S(1)} %broadcast_select_fusion.11), channel_id=1, source_target_pairs={{0,8},{16,24}} | collective-permute-start | bytes 786440 | tf_op jit(solution)/shard_map/ppermute | solution.py:190
  13.5 1.4 %collective-permute-start.3 = (f32[128,768]{1,0:T(8,128)S(1)}, f32[128,768]{1,0:T(8,128)}, u32[]{:S(2)}, u32[]{:S(2)}) collective-permute-start(f32[128,768]{1,0:T(8,128)S(1)} %pad_maximum_fusion), channel_id=1, source_target_pairs={{0,4}} | collective-permute-start | bytes 1179656 | tf_op jit(solution)/shard_map/ppermute | solution.py:190
  14.9 1.6 %collective-permute-done.1 = f32[128,512]{1,0:T(8,128)} collective-permute-done((f32[128,512]{1,0:T(8,128)S(1)}, f32[128,512]{1,0:T(8,128)}, u32[]{:S(2)}, u32[]{:S(2)}) %collective-permute-start.1) | collective-permute-done | bytes 262176 | tf_op jit(solution)/shard_map/ppermute | solution.py:190
  16.6 1.3 %collective-permute-start.2 = (f32[128,512]{1,0:T(8,128)S(1)}, f32[128,512]{1,0:T(8,128)S(1)}, u32[]{:S(2)}, u32[]{:S(2)}) collective-permute-start(f32[128,512]{1,0:T(8,128)S(1)} %broadcast_select_fusion.12), channel_id=1, source_target_pairs={{0,4},{16,20},{8,12},{24,28}} | collective-permute-start | bytes 786440 | tf_op jit(solution)/shard_map/ppermute | solution.py:190
  18.0 3.7 %collective-permute-done.2 = f32[128,512]{1,0:T(8,128)S(1)} collective-permute-done((f32[128,512]{1,0:T(8,128)S(1)}, f32[128,512]{1,0:T(8,128)S(1)}, u32[]{:S(2)}, u32[]{:S(2)}) %collective-permute-start.2) | collective-permute-done | bytes 262176 | tf_op jit(solution)/shard_map/ppermute | solution.py:190
  22.7 2.3 %collective-permute-start.5 = (f32[512,512]{1,0:T(8,128)S(1)}, f32[512,512]{1,0:T(8,128)}, u32[]{:S(2)}, u32[]{:S(2)}) collective-permute-start(f32[512,512]{1,0:T(8,128)S(1)} %broadcast_select_fusion.2), channel_id=1, source_target_pairs={{0,1},{2,3},{4,5},{6,7},{8,9},{10,11},{12,13},{14,15},{16,17},{18,... | collective-permute-start | bytes 3145736 | tf_op jit(solution)/shard_map/ppermute | solution.py:190
  25.0 1.4 %collective-permute-start.8 = (f32[128,768]{1,0:T(8,128)S(1)}, f32[128,768]{1,0:T(8,128)S(1)}, u32[]{:S(2)}, u32[]{:S(2)}) collective-permute-start(f32[128,768]{1,0:T(8,128)S(1)} %broadcast_select_fusion.8), channel_id=1, source_target_pairs={{0,16},{4,20}} | collective-permute-start | bytes 1179656 | tf_op jit(solution)/shard_map/ppermute | solution.py:190
  26.4 3.3 %collective-permute-start.6 = (f32[128,512]{1,0:T(8,128)}, f32[128,512]{1,0:T(8,128)S(1)}, u32[]{:S(2)}, u32[]{:S(2)}) collective-permute-start(f32[128,512]{1,0:T(8,128)} %broadcast_select_fusion.13), channel_id=1, source_target_pairs={{0,2},{4,6},{8,10},{12,14},{16,18},{20,22},{24,26},{28,30}} | collective-permute-start | bytes 786440 | tf_op jit(solution)/shard_map/ppermute | solution.py:190
  29.7 1.4 %broadcast_select_fusion.3 = f32[512,512]{1,0:T(8,128)S(1)} fusion(f32[512,512]{1,0:T(8,128)} %collective-permute-done.5, f32[512,512]{1,0:T(8,128)} %copy-done.3, pred[]{:T(512)S(6)} %eq.61), kind=kLoop, calls=%fused_computation.9 | loop fusion | flops 262144 | bytes 3145729 | tf_op jit(solution)/shard_map/jit(_where)/select_n | solution.py:191
  31.2 1.7 %collective-permute-start.10 = (f32[512,512]{1,0:T(8,128)S(1)}, f32[512,512]{1,0:T(8,128)}, u32[]{:S(2)}, u32[]{:S(2)}) collective-permute-start(f32[512,512]{1,0:T(8,128)S(1)} %broadcast_select_fusion.3), channel_id=1, source_target_pairs={{0,8},{4,12},{9,17},{13,21},{18,26},{22,30},{27,3},{31,7}} | collective-permute-start | bytes 3145736 | tf_op jit(solution)/shard_map/ppermute | solution.py:242
  34.6 2.0 %collective-permute-start.7 = (f32[128,512]{1,0:T(8,128)}, f32[128,512]{1,0:T(8,128)}, u32[]{:S(2)}, u32[]{:S(2)}) collective-permute-start(f32[128,512]{1,0:T(8,128)} %broadcast_select_fusion.9), channel_id=1, source_target_pairs={{0,1},{4,5},{8,9},{12,13},{16,17},{20,21},{24,25},{28,29},{2,3},{6... | collective-permute-start | bytes 786440 | tf_op jit(solution)/shard_map/ppermute | solution.py:190
  37.4 4.2 %collective-permute-start.9 = (f32[128,768]{1,0:T(8,128)}, f32[128,768]{1,0:T(8,128)}, u32[]{:S(2)}, u32[]{:S(2)}) collective-permute-start(f32[128,768]{1,0:T(8,128)} %broadcast_select_fusion.6), channel_id=1, source_target_pairs={{0,8},{4,12},{16,24},{20,28}} | collective-permute-start | bytes 1179656 | tf_op jit(solution)/shard_map/ppermute | solution.py:190
  41.7 1.7 %broadcast_select_fusion.10.top_ref = f32[128,512]{1,0:T(8,128)} fusion(f32[128,512]{1,0:T(8,128)} %collective-permute-done.7, f32[128,512]{1,0:T(8,128)} %broadcast_select_fusion.9, pred[]{:T(512)S(6)} %eq.66), kind=kLoop, calls=%fused_computation.17 | loop fusion | flops 65536 | bytes 786433 | tf_op jit(solution)/shard_map/jit(_where)/select_n | solution.py:191
  43.4 3.1 %collective-permute-done.9 = f32[128,768]{1,0:T(8,128)} collective-permute-done((f32[128,768]{1,0:T(8,128)}, f32[128,768]{1,0:T(8,128)}, u32[]{:S(2)}, u32[]{:S(2)}) %collective-permute-start.9) | collective-permute-done | bytes 393248 | tf_op jit(solution)/shard_map/ppermute | solution.py:190
  50.1 2.4 %collective-permute-start.11 = (f32[128,768]{1,0:T(8,128)S(1)}, f32[128,768]{1,0:T(8,128)}, u32[]{:S(2)}, u32[]{:S(2)}) collective-permute-start(f32[128,768]{1,0:T(8,128)S(1)} %broadcast_select_fusion.7), channel_id=1, source_target_pairs={{0,2},{4,6},{16,18},{20,22},{8,10},{12,14},{24,26},{28,30}} | collective-permute-start | bytes 1179656 | tf_op jit(solution)/shard_map/ppermute | solution.py:190
  52.4 8.8 %first_panel.1 = (f32[128,512]{1,0:T(8,128)}, f32[128,128]{1,0:T(8,128)}, f32[8,128]{1,0:T(8,128)}) custom-call(f32[128,512]{1,0:T(8,128)} %broadcast_select_fusion.10.top_ref), custom_call_target="tpu_custom_call" | custom-call | tf_op jit(solution)/shard_map/first_panel/pallas_call | solution.py:125
  62.2 17.6 %collective-permute-done.12 = f32[512,512]{1,0:T(8,128)} collective-permute-done((f32[512,512]{1,0:T(8,128)}, f32[512,512]{1,0:T(8,128)}, u32[]{:S(2)}, u32[]{:S(2)}) %collective-permute-start.12) | collective-permute-done | bytes 1048608 | tf_op jit(solution)/shard_map/ppermute | solution.py:242
  79.9 2.4 %broadcast_select_fusion = f32[512,512]{1,0:T(8,128)} fusion(f32[512,512]{1,0:T(8,128)} %collective-permute-done.12, f32[512,512]{1,0:T(8,128)} %broadcast_select_fusion.1, pred[]{:T(512)S(6)} %or.11), kind=kLoop, calls=%fused_computation.6 | loop fusion | flops 262144 | bytes 3145729 | tf_op jit(solution)/shard_map/jit(_where)/select_n | solution.py:259
  82.3 1.9 %collective-permute-start.14 = (f32[512,512]{1,0:T(8,128)}, f32[512,512]{1,0:T(8,128)}, u32[]{:S(2)}, u32[]{:S(2)}) collective-permute-start(f32[512,512]{1,0:T(8,128)} %broadcast_select_fusion), channel_id=1, source_target_pairs={{0,4},{4,0},{8,12},{12,8},{16,20},{20,16},{24,28},{28,24},{1,5},{5... | collective-permute-start | bytes 3145736 | tf_op jit(solution)/shard_map/ppermute | solution.py:270
  84.1 2.0 %collective-permute-start.13 = (f32[128,768]{1,0:T(8,128)S(1)}, f32[128,768]{1,0:T(8,128)}, u32[]{:S(2)}, u32[]{:S(2)}) collective-permute-start(f32[128,768]{1,0:T(8,128)S(1)} %broadcast_select_fusion.5), channel_id=1, source_target_pairs={{0,1},{4,5},{16,17},{20,21},{8,9},{12,13},{24,25},{28,29},{2,3},{6... | collective-permute-start | bytes 1179656 | tf_op jit(solution)/shard_map/ppermute | solution.py:190
  86.2 1.8 %copy.3 = f32[512,1024]{0,1:T(8,128)} copy(f32[512,1024]{1,0:T(8,128)S(1)} %copy-done) | data formatting | bytes 4194304 | tf_op args[0]
  88.2 1.3 %bitcast_dynamic-update-slice_fusion.1 = f32[2,512,512]{2,1,0:T(8,128)S(1)} fusion(f32[2,512,512]{2,1,0:T(8,128)S(1)} %broadcast_in_dim.30, s32[]{:T(128)S(6)} %select_n.249, f32[512,512]{1,0:T(8,128)} %broadcast_select_fusion), kind=kLoop, calls=%fused_computation.2 | loop fusion | bytes 2097156 | tf_op jit(solution)/shard_map/dynamic_update_slice | solution.py:267
  90.4 25.3 %other_panels.1 = (f32[512,512]{1,0:T(8,128)}, f32[8,128]{1,0:T(8,128)}) custom-call(f32[128,512]{1,0:T(8,128)} %get-tuple-element.23.top_ref, f32[128,128]{1,0:T(8,128)} %get-tuple-element.24.inv_ref, f32[8,128]{1,0:T(8,128)} %get-tuple-element.25.log_ref, f32[128,768]{1,0:T(8,128)} %broadcast_select_fusion.4.rest_ref), custom_call_target="tpu_custom_call" | custom-call | tf_op jit(solution)/shard_map/other_panels/pallas_call | solution.py:172
  116.8 2.2 %fusion.1 = (f32[512,512]{0,1:T(8,128)S(1)}, f32[512,512]{0,1:T(8,128)S(1)}) fusion(pred[]{:T(512)S(6)} %gt.4, f32[512,512]{1,0:T(8,128)S(1)} %broadcast_select_fusion.3, f32[512,512]{1,0:T(8,128)} %get-tuple-element.27), kind=kOutput, calls=%fused_computation.5 | convolution fusion | flops 806092800 | bytes 4194305 | tf_op jit(solution)/shard_map/dot_general | solution.py:277
  119.1 1.4 %bitcast_dynamic-update-slice_fusion = f32[2,512,512]{2,1,0:T(8,128)S(1)} fusion(f32[2,512,512]{2,1,0:T(8,128)S(1)} %bitcast_dynamic-update-slice_fusion.1, s32[]{:T(128)S(6)} %select_n.251, f32[512,512]{1,0:T(8,128)} %collective-permute-done.14), kind=kLoop, calls=%fused_computation.1 | loop fusion | bytes 2097156 | tf_op jit(solution)/shard_map/dynamic_update_slice | solution.py:271
  120.6 1.9 %fusion.7 = f32[1024,512]{1,0:T(8,128)S(1)} fusion(f32[1024,512]{1,0:T(8,128)S(1)} %bitcast.12, f32[512,512]{1,0:T(8,128)S(1)} %copy-done.2), kind=kOutput, calls=%fused_computation.30 | convolution fusion | flops 1610612736 | bytes 5242880 | tf_op jit(solution)/shard_map/dot_general | solution.py:278
  122.5 2.0 %maximum_select_fusion = f32[512,1024]{0,1:T(8,128)S(1)} fusion(f32[512,512]{0,1:T(8,128)S(1)} %get-tuple-element.32, f32[512,1024]{0,1:T(8,128)S(1)} %copy-done.1, f32[512,512]{0,1:T(8,128)S(1)} %get-tuple-element.33, f32[1024,512]{1,0:T(8,128)S(1)} %fusion.7, pred[1024]{0:T(1024)(128)(4,1)S(1)} %fusion.3, pred[]{:T(512)S(6)} %gt.4), kind=kOutput, calls=%fused_computation | convolution fusion | flops 1612709888 | bytes 8389633 | tf_op jit(solution)/shard_map/dot_general | solution.py:279
  124.5 1.8 %copy.5 = f32[512,1024]{1,0:T(8,128)} copy(f32[512,1024]{0,1:T(8,128)S(1)} %maximum_select_fusion) | data formatting | bytes 4194304
  (42 shorter events, 11.8 us)
Async XLA Ops:
  0.6 10.3 %copy-start = (f32[512,1024]{1,0:T(8,128)S(1)}, f32[512,1024]{1,0:T(8,128)}, u32[]{:S(2)}) copy-start(f32[512,1024]{1,0:T(8,128)} %param.1) | copy-start | bytes 6291460
  1.8 9.2 %collective-permute-start = (f32[128,512]{1,0:T(8,128)S(1)}, f32[128,512]{1,0:T(8,128)S(1)}, u32[]{:S(2)}, u32[]{:S(2)}) collective-permute-start(f32[128,512]{1,0:T(8,128)S(1)} %slice.18), channel_id=1, source_target_pairs={{0,16}} | collective-permute-start | bytes 786440 | tf_op jit(solution)/shard_map/ppermute | solution.py:190
  5.3 17.2 %collective-permute-start.4 = (f32[512,512]{1,0:T(8,128)}, f32[512,512]{1,0:T(8,128)}, u32[]{:S(2)}, u32[]{:S(2)}) collective-permute-start(f32[512,512]{1,0:T(8,128)} %slice.22), channel_id=1, source_target_pairs={{0,2},{4,6},{8,10},{12,14},{16,18},{20,22},{24,26},{28,30}} | collective-permute-start | bytes 3145736 | tf_op jit(solution)/shard_map/ppermute | solution.py:190
  11.0 5.6 %collective-permute-start.1 = (f32[128,512]{1,0:T(8,128)S(1)}, f32[128,512]{1,0:T(8,128)}, u32[]{:S(2)}, u32[]{:S(2)}) collective-permute-start(f32[128,512]{1,0:T(8,128)S(1)} %broadcast_select_fusion.11), channel_id=1, source_target_pairs={{0,8},{16,24}} | collective-permute-start | bytes 786440 | tf_op jit(solution)/shard_map/ppermute | solution.py:190
  13.5 4.5 %collective-permute-start.3 = (f32[128,768]{1,0:T(8,128)S(1)}, f32[128,768]{1,0:T(8,128)}, u32[]{:S(2)}, u32[]{:S(2)}) collective-permute-start(f32[128,768]{1,0:T(8,128)S(1)} %pad_maximum_fusion), channel_id=1, source_target_pairs={{0,4}} | collective-permute-start | bytes 1179656 | tf_op jit(solution)/shard_map/ppermute | solution.py:190
  16.6 5.2 %collective-permute-start.2 = (f32[128,512]{1,0:T(8,128)S(1)}, f32[128,512]{1,0:T(8,128)S(1)}, u32[]{:S(2)}, u32[]{:S(2)}) collective-permute-start(f32[128,512]{1,0:T(8,128)S(1)} %broadcast_select_fusion.12), channel_id=1, source_target_pairs={{0,4},{16,20},{8,12},{24,28}} | collective-permute-start | bytes 786440 | tf_op jit(solution)/shard_map/ppermute | solution.py:190
  22.7 7.0 %copy-start.3 = (f32[512,512]{1,0:T(8,128)}, f32[512,512]{1,0:T(8,128)S(1)}, u32[]{:S(2)}) copy-start(f32[512,512]{1,0:T(8,128)S(1)} %broadcast_select_fusion.2) | copy-start | bytes 3145732
  22.7 7.0 %collective-permute-start.5 = (f32[512,512]{1,0:T(8,128)S(1)}, f32[512,512]{1,0:T(8,128)}, u32[]{:S(2)}, u32[]{:S(2)}) collective-permute-start(f32[512,512]{1,0:T(8,128)S(1)} %broadcast_select_fusion.2), channel_id=1, source_target_pairs={{0,1},{2,3},{4,5},{6,7},{8,9},{10,11},{12,13},{14,15},{16,17},{18,... | collective-permute-start | bytes 3145736 | tf_op jit(solution)/shard_map/ppermute | solution.py:190
  25.0 8.9 %copy-start.5 = (f32[128,512]{1,0:T(8,128)S(1)}, f32[128,512]{1,0:T(8,128)}, u32[]{:S(2)}) copy-start(f32[128,512]{1,0:T(8,128)} %broadcast_select_fusion.13) | copy-start | bytes 786436
  25.0 11.6 %collective-permute-start.8 = (f32[128,768]{1,0:T(8,128)S(1)}, f32[128,768]{1,0:T(8,128)S(1)}, u32[]{:S(2)}, u32[]{:S(2)}) collective-permute-start(f32[128,768]{1,0:T(8,128)S(1)} %broadcast_select_fusion.8), channel_id=1, source_target_pairs={{0,16},{4,20}} | collective-permute-start | bytes 1179656 | tf_op jit(solution)/shard_map/ppermute | solution.py:190
  26.4 7.5 %collective-permute-start.6 = (f32[128,512]{1,0:T(8,128)}, f32[128,512]{1,0:T(8,128)S(1)}, u32[]{:S(2)}, u32[]{:S(2)}) collective-permute-start(f32[128,512]{1,0:T(8,128)} %broadcast_select_fusion.13), channel_id=1, source_target_pairs={{0,2},{4,6},{8,10},{12,14},{16,18},{20,22},{24,26},{28,30}} | collective-permute-start | bytes 786440 | tf_op jit(solution)/shard_map/ppermute | solution.py:190
  31.2 16.4 %collective-permute-start.10 = (f32[512,512]{1,0:T(8,128)S(1)}, f32[512,512]{1,0:T(8,128)}, u32[]{:S(2)}, u32[]{:S(2)}) collective-permute-start(f32[512,512]{1,0:T(8,128)S(1)} %broadcast_select_fusion.3), channel_id=1, source_target_pairs={{0,8},{4,12},{9,17},{13,21},{18,26},{22,30},{27,3},{31,7}} | collective-permute-start | bytes 3145736 | tf_op jit(solution)/shard_map/ppermute | solution.py:242
  34.6 7.0 %collective-permute-start.7 = (f32[128,512]{1,0:T(8,128)}, f32[128,512]{1,0:T(8,128)}, u32[]{:S(2)}, u32[]{:S(2)}) collective-permute-start(f32[128,512]{1,0:T(8,128)} %broadcast_select_fusion.9), channel_id=1, source_target_pairs={{0,1},{4,5},{8,9},{12,13},{16,17},{20,21},{24,25},{28,29},{2,3},{6... | collective-permute-start | bytes 786440 | tf_op jit(solution)/shard_map/ppermute | solution.py:190
  37.4 9.1 %collective-permute-start.9 = (f32[128,768]{1,0:T(8,128)}, f32[128,768]{1,0:T(8,128)}, u32[]{:S(2)}, u32[]{:S(2)}) collective-permute-start(f32[128,768]{1,0:T(8,128)} %broadcast_select_fusion.6), channel_id=1, source_target_pairs={{0,8},{4,12},{16,24},{20,28}} | collective-permute-start | bytes 1179656 | tf_op jit(solution)/shard_map/ppermute | solution.py:190
  47.6 13.6 %copy-start.4 = (f32[128,768]{1,0:T(8,128)}, f32[128,768]{1,0:T(8,128)S(1)}, u32[]{:S(2)}) copy-start(f32[128,768]{1,0:T(8,128)S(1)} %broadcast_select_fusion.7) | copy-start | bytes 1179652
  48.8 31.1 %collective-permute-start.12 = (f32[512,512]{1,0:T(8,128)}, f32[512,512]{1,0:T(8,128)}, u32[]{:S(2)}, u32[]{:S(2)}) collective-permute-start(f32[512,512]{1,0:T(8,128)} %broadcast_select_fusion.1), channel_id=1, source_target_pairs={{0,24},{8,16},{4,28},{12,20},{9,1},{17,25},{13,5},{21,29},{18,10},... | collective-permute-start | bytes 3145736 | tf_op jit(solution)/shard_map/ppermute | solution.py:242
  50.1 11.1 %collective-permute-start.11 = (f32[128,768]{1,0:T(8,128)S(1)}, f32[128,768]{1,0:T(8,128)}, u32[]{:S(2)}, u32[]{:S(2)}) collective-permute-start(f32[128,768]{1,0:T(8,128)S(1)} %broadcast_select_fusion.7), channel_id=1, source_target_pairs={{0,2},{4,6},{16,18},{20,22},{8,10},{12,14},{24,26},{28,30}} | collective-permute-start | bytes 1179656 | tf_op jit(solution)/shard_map/ppermute | solution.py:190
  82.3 36.8 %collective-permute-start.14 = (f32[512,512]{1,0:T(8,128)}, f32[512,512]{1,0:T(8,128)}, u32[]{:S(2)}, u32[]{:S(2)}) collective-permute-start(f32[512,512]{1,0:T(8,128)} %broadcast_select_fusion), channel_id=1, source_target_pairs={{0,4},{4,0},{8,12},{12,8},{16,20},{20,16},{24,28},{28,24},{1,5},{5... | collective-permute-start | bytes 3145736 | tf_op jit(solution)/shard_map/ppermute | solution.py:270
  84.1 5.4 %collective-permute-start.13 = (f32[128,768]{1,0:T(8,128)S(1)}, f32[128,768]{1,0:T(8,128)}, u32[]{:S(2)}, u32[]{:S(2)}) collective-permute-start(f32[128,768]{1,0:T(8,128)S(1)} %broadcast_select_fusion.5), channel_id=1, source_target_pairs={{0,1},{4,5},{16,17},{20,21},{8,9},{12,13},{24,25},{28,29},{2,3},{6... | collective-permute-start | bytes 1179656 | tf_op jit(solution)/shard_map/ppermute | solution.py:190
  119.1 1.5 %copy-start.2 = (f32[512,512]{1,0:T(8,128)S(1)}, f32[512,512]{1,0:T(8,128)}, u32[]{:S(2)}) copy-start(f32[512,512]{1,0:T(8,128)} %get-tuple-element.27) | copy-start | bytes 3145732
  120.6 1.9 %copy-start.1 = (f32[512,1024]{0,1:T(8,128)S(1)}, f32[512,1024]{0,1:T(8,128)}, u32[]{:S(2)}) copy-start(f32[512,1024]{0,1:T(8,128)} %copy.3) | copy-start | bytes 6291460

commit v4 on v3

--- a/solution.py
+++ b/solution.py
@@ -261,8 +261,9 @@
 
     rest = tree_rounds(rest, both, order[-2:-1], reach(order[:-2]))
     top, inv, log = first_panel(first, count)
-    top, rest, far = lax.optimization_barrier((top, rest, far))
+    top, rest = lax.optimization_barrier((top, rest))
     rest = tree_rounds(rest, both, order[-1:], reach(order[:-1]))
+    top, far = lax.optimization_barrier((top, far))
     parts = jnp.zeros((per_col, width, width), jnp.float32)
     parts = lax.dynamic_update_slice(parts, far[None], (row % per_col, 0, 0))
     for s in range(1, per_col):

time: 127 us -> 124 us (0.976)
  waiting for transfers between devices: 29 us -> 25.8 us
    ppermute x2, waiting for transfers between devices: 17.6 us -> 14.5 us  [per_device(): lax.ppermute(far, both, [(((c + src) % cols_n * per_col + b) * cols_n + c...]
  transfers between devices with their start and end apart: 15 -> 15, of which waited for: 6 -> 6; matrix products, arithmetic and copies ran while one was open for 14% -> 15% of each run, Pallas kernels for 27% -> 28%
where the time goes in v4:
time: 124 us; the launch traced here: 123 us
  Pallas kernels  34 us (27%)
  starting transfers between devices  33.8 us (27%)
  waiting for transfers between devices  25.8 us (21%)
  other arithmetic  12.3 us (10%)
  local copies, waits for them, and re-layouts  11.2 us (9%)
  matrix products  4.9 us (4%)
    ppermute x12, starting transfers between devices, tree_rounds(): got = lax.ppermute(value, axes, [(s, s + stride) for s in have])  29 us
    pallas_call x1, Pallas kernels, other_panels(): pl.pallas_call(body, out_shape=[jax.ShapeDtypeStruct((count * LANES, coun...  25.3 us
    ppermute x2, waiting for transfers between devices, per_device(): lax.ppermute(far, both, [(((c + src) % cols_n * per_col + b) * cols_n + c...  14.5 us
    ppermute x12, waiting for transfers between devices, tree_rounds(): got = lax.ppermute(value, axes, [(s, s + stride) for s in have])  11.3 us
    pallas_call x1, Pallas kernels, first_panel(): pl.pallas_call(body, out_shape=[jax.ShapeDtypeStruct((LANES, count * LANE...  8.75 us
    select_n x12, other arithmetic, tree_rounds(): value = jnp.where(index // stride % 2 == 1, got, value)  8.64 us
    unnamed x14, local copies, waits for them, and re-layouts  3.65 us
    select_n x2, other arithmetic, per_device(): far = jnp.where(takes, got, far)  3.62 us
  transfers between devices with their start and end apart: 15, of which 6 were waited for; matrix products, arithmetic and copies ran while one was open for 15% of the time, Pallas kernels for 28%

profile of v4, /device:TPU:16, one launch (start us, length us, event | category | flops | bytes accessed | tf_op | source)
XLA Modules:
  0.0 122.9 jit_solution(2926654969979861763)
XLA Ops:
  1.8 1.3 %collective-permute-start = (f32[128,512]{1,0:T(8,128)S(1)}, f32[128,512]{1,0:T(8,128)S(1)}, u32[]{:S(2)}, u32[]{:S(2)}) collective-permute-start(f32[128,512]{1,0:T(8,128)S(1)} %slice.18), channel_id=1, source_target_pairs={{0,16}} | collective-permute-start | bytes 786440 | tf_op jit(solution)/shard_map/ppermute | solution.py:190
  3.1 2.3 %slice.22 = f32[512,512]{1,0:T(8,128)} slice(f32[512,1024]{1,0:T(8,128)} %param.1), slice={[0:512], [0:512]} | slice | bytes 2097152 | tf_op jit(solution)/shard_map/slice | solution.py:228
  5.3 3.8 %collective-permute-start.4 = (f32[512,512]{1,0:T(8,128)}, f32[512,512]{1,0:T(8,128)}, u32[]{:S(2)}, u32[]{:S(2)}) collective-permute-start(f32[512,512]{1,0:T(8,128)} %slice.22), channel_id=1, source_target_pairs={{0,2},{4,6},{8,10},{12,14},{16,18},{20,22},{24,26},{28,30}} | collective-permute-start | bytes 3145736 | tf_op jit(solution)/shard_map/ppermute | solution.py:190
  9.1 1.8 %collective-permute-done = f32[128,512]{1,0:T(8,128)S(1)} collective-permute-done((f32[128,512]{1,0:T(8,128)S(1)}, f32[128,512]{1,0:T(8,128)S(1)}, u32[]{:S(2)}, u32[]{:S(2)}) %collective-permute-start) | collective-permute-done | bytes 262176 | tf_op jit(solution)/shard_map/ppermute | solution.py:190
  11.0 2.4 %collective-permute-start.1 = (f32[128,512]{1,0:T(8,128)S(1)}, f32[128,512]{1,0:T(8,128)}, u32[]{:S(2)}, u32[]{:S(2)}) collective-permute-start(f32[128,512]{1,0:T(8,128)S(1)} %broadcast_select_fusion.11), channel_id=1, source_target_pairs={{0,8},{16,24}} | collective-permute-start | bytes 786440 | tf_op jit(solution)/shard_map/ppermute | solution.py:190
  13.5 1.4 %collective-permute-start.3 = (f32[128,768]{1,0:T(8,128)S(1)}, f32[128,768]{1,0:T(8,128)}, u32[]{:S(2)}, u32[]{:S(2)}) collective-permute-start(f32[128,768]{1,0:T(8,128)S(1)} %pad_maximum_fusion), channel_id=1, source_target_pairs={{0,4}} | collective-permute-start | bytes 1179656 | tf_op jit(solution)/shard_map/ppermute | solution.py:190
  14.9 1.6 %collective-permute-done.1 = f32[128,512]{1,0:T(8,128)} collective-permute-done((f32[128,512]{1,0:T(8,128)S(1)}, f32[128,512]{1,0:T(8,128)}, u32[]{:S(2)}, u32[]{:S(2)}) %collective-permute-start.1) | collective-permute-done | bytes 262176 | tf_op jit(solution)/shard_map/ppermute | solution.py:190
  16.6 1.3 %collective-permute-start.2 = (f32[128,512]{1,0:T(8,128)S(1)}, f32[128,512]{1,0:T(8,128)S(1)}, u32[]{:S(2)}, u32[]{:S(2)}) collective-permute-start(f32[128,512]{1,0:T(8,128)S(1)} %broadcast_select_fusion.12), channel_id=1, source_target_pairs={{0,4},{16,20},{8,12},{24,28}} | collective-permute-start | bytes 786440 | tf_op jit(solution)/shard_map/ppermute | solution.py:190
  18.0 3.7 %collective-permute-done.2 = f32[128,512]{1,0:T(8,128)S(1)} collective-permute-done((f32[128,512]{1,0:T(8,128)S(1)}, f32[128,512]{1,0:T(8,128)S(1)}, u32[]{:S(2)}, u32[]{:S(2)}) %collective-permute-start.2) | collective-permute-done | bytes 262176 | tf_op jit(solution)/shard_map/ppermute | solution.py:190
  22.7 2.3 %collective-permute-start.5 = (f32[512,512]{1,0:T(8,128)S(1)}, f32[512,512]{1,0:T(8,128)}, u32[]{:S(2)}, u32[]{:S(2)}) collective-permute-start(f32[512,512]{1,0:T(8,128)S(1)} %broadcast_select_fusion.2), channel_id=1, source_target_pairs={{0,1},{2,3},{4,5},{6,7},{8,9},{10,11},{12,13},{14,15},{16,17},{18,... | collective-permute-start | bytes 3145736 | tf_op jit(solution)/shard_map/ppermute | solution.py:190
  25.0 1.4 %collective-permute-start.8 = (f32[128,768]{1,0:T(8,128)S(1)}, f32[128,768]{1,0:T(8,128)S(1)}, u32[]{:S(2)}, u32[]{:S(2)}) collective-permute-start(f32[128,768]{1,0:T(8,128)S(1)} %broadcast_select_fusion.8), channel_id=1, source_target_pairs={{0,16},{4,20}} | collective-permute-start | bytes 1179656 | tf_op jit(solution)/shard_map/ppermute | solution.py:190
  26.4 3.3 %collective-permute-start.6 = (f32[128,512]{1,0:T(8,128)}, f32[128,512]{1,0:T(8,128)S(1)}, u32[]{:S(2)}, u32[]{:S(2)}) collective-permute-start(f32[128,512]{1,0:T(8,128)} %broadcast_select_fusion.13), channel_id=1, source_target_pairs={{0,2},{4,6},{8,10},{12,14},{16,18},{20,22},{24,26},{28,30}} | collective-permute-start | bytes 786440 | tf_op jit(solution)/shard_map/ppermute | solution.py:190
  29.7 1.4 %broadcast_select_fusion.3 = f32[512,512]{1,0:T(8,128)S(1)} fusion(f32[512,512]{1,0:T(8,128)} %collective-permute-done.5, f32[512,512]{1,0:T(8,128)} %copy-done.3, pred[]{:T(512)S(6)} %eq.61), kind=kLoop, calls=%fused_computation.9 | loop fusion | flops 262144 | bytes 3145729 | tf_op jit(solution)/shard_map/jit(_where)/select_n | solution.py:191
  31.2 1.7 %collective-permute-start.10 = (f32[512,512]{1,0:T(8,128)S(1)}, f32[512,512]{1,0:T(8,128)}, u32[]{:S(2)}, u32[]{:S(2)}) collective-permute-start(f32[512,512]{1,0:T(8,128)S(1)} %broadcast_select_fusion.3), channel_id=1, source_target_pairs={{0,8},{4,12},{9,17},{13,21},{18,26},{22,30},{27,3},{31,7}} | collective-permute-start | bytes 3145736 | tf_op jit(solution)/shard_map/ppermute | solution.py:242
  34.6 2.0 %collective-permute-start.7 = (f32[128,512]{1,0:T(8,128)}, f32[128,512]{1,0:T(8,128)}, u32[]{:S(2)}, u32[]{:S(2)}) collective-permute-start(f32[128,512]{1,0:T(8,128)} %broadcast_select_fusion.9), channel_id=1, source_target_pairs={{0,1},{4,5},{8,9},{12,13},{16,17},{20,21},{24,25},{28,29},{2,3},{6... | collective-permute-start | bytes 786440 | tf_op jit(solution)/shard_map/ppermute | solution.py:190
  37.4 4.2 %collective-permute-start.9 = (f32[128,768]{1,0:T(8,128)}, f32[128,768]{1,0:T(8,128)}, u32[]{:S(2)}, u32[]{:S(2)}) collective-permute-start(f32[128,768]{1,0:T(8,128)} %broadcast_select_fusion.6), channel_id=1, source_target_pairs={{0,8},{4,12},{16,24},{20,28}} | collective-permute-start | bytes 1179656 | tf_op jit(solution)/shard_map/ppermute | solution.py:190
  41.7 1.7 %broadcast_select_fusion.10.top_ref = f32[128,512]{1,0:T(8,128)} fusion(f32[128,512]{1,0:T(8,128)} %collective-permute-done.7, f32[128,512]{1,0:T(8,128)} %broadcast_select_fusion.9, pred[]{:T(512)S(6)} %eq.66), kind=kLoop, calls=%fused_computation.17 | loop fusion | flops 65536 | bytes 786433 | tf_op jit(solution)/shard_map/jit(_where)/select_n | solution.py:191
  43.4 3.1 %collective-permute-done.9 = f32[128,768]{1,0:T(8,128)} collective-permute-done((f32[128,768]{1,0:T(8,128)}, f32[128,768]{1,0:T(8,128)}, u32[]{:S(2)}, u32[]{:S(2)}) %collective-permute-start.9) | collective-permute-done | bytes 393248 | tf_op jit(solution)/shard_map/ppermute | solution.py:190
  48.8 1.3 %collective-permute-start.12 = (f32[512,512]{1,0:T(8,128)}, f32[512,512]{1,0:T(8,128)}, u32[]{:S(2)}, u32[]{:S(2)}) collective-permute-start(f32[512,512]{1,0:T(8,128)} %broadcast_select_fusion.1), channel_id=1, source_target_pairs={{0,24},{8,16},{4,28},{12,20},{9,1},{17,25},{13,5},{21,29},{18,10},... | collective-permute-start | bytes 3145736 | tf_op jit(solution)/shard_map/ppermute | solution.py:242
  50.1 2.4 %collective-permute-start.11 = (f32[128,768]{1,0:T(8,128)S(1)}, f32[128,768]{1,0:T(8,128)}, u32[]{:S(2)}, u32[]{:S(2)}) collective-permute-start(f32[128,768]{1,0:T(8,128)S(1)} %broadcast_select_fusion.7), channel_id=1, source_target_pairs={{0,2},{4,6},{16,18},{20,22},{8,10},{12,14},{24,26},{28,30}} | collective-permute-start | bytes 1179656 | tf_op jit(solution)/shard_map/ppermute | solution.py:190
  52.4 8.8 %first_panel.1 = (f32[128,512]{1,0:T(8,128)}, f32[128,128]{1,0:T(8,128)}, f32[8,128]{1,0:T(8,128)}) custom-call(f32[128,512]{1,0:T(8,128)} %broadcast_select_fusion.10.top_ref), custom_call_target="tpu_custom_call" | custom-call | tf_op jit(solution)/shard_map/first_panel/pallas_call | solution.py:125
  62.2 3.1 %collective-permute-start.13 = (f32[128,768]{1,0:T(8,128)S(1)}, f32[128,768]{1,0:T(8,128)}, u32[]{:S(2)}, u32[]{:S(2)}) collective-permute-start(f32[128,768]{1,0:T(8,128)S(1)} %broadcast_select_fusion.5), channel_id=1, source_target_pairs={{0,1},{4,5},{16,17},{20,21},{8,9},{12,13},{24,25},{28,29},{2,3},{6... | collective-permute-start | bytes 1179656 | tf_op jit(solution)/shard_map/ppermute | solution.py:190
  65.4 14.5 %collective-permute-done.12 = f32[512,512]{1,0:T(8,128)} collective-permute-done((f32[512,512]{1,0:T(8,128)}, f32[512,512]{1,0:T(8,128)}, u32[]{:S(2)}, u32[]{:S(2)}) %collective-permute-start.12) | collective-permute-done | bytes 1048608 | tf_op jit(solution)/shard_map/ppermute | solution.py:242
  79.9 2.4 %broadcast_select_fusion = f32[512,512]{1,0:T(8,128)} fusion(f32[512,512]{1,0:T(8,128)} %collective-permute-done.12, f32[512,512]{1,0:T(8,128)} %broadcast_select_fusion.1, pred[]{:T(512)S(6)} %or.11), kind=kLoop, calls=%fused_computation.6 | loop fusion | flops 262144 | bytes 3145729 | tf_op jit(solution)/shard_map/jit(_where)/select_n | solution.py:259
  82.3 1.9 %collective-permute-start.14 = (f32[512,512]{1,0:T(8,128)}, f32[512,512]{1,0:T(8,128)}, u32[]{:S(2)}, u32[]{:S(2)}) collective-permute-start(f32[512,512]{1,0:T(8,128)} %broadcast_select_fusion), channel_id=1, source_target_pairs={{0,4},{4,0},{8,12},{12,8},{16,20},{20,16},{24,28},{28,24},{1,5},{5... | collective-permute-start | bytes 3145736 | tf_op jit(solution)/shard_map/ppermute | solution.py:271
  84.1 1.8 %copy.3 = f32[512,1024]{0,1:T(8,128)} copy(f32[512,1024]{1,0:T(8,128)S(1)} %copy-done) | data formatting | bytes 4194304 | tf_op args[0]
  86.8 25.3 %other_panels.1 = (f32[512,512]{1,0:T(8,128)}, f32[8,128]{1,0:T(8,128)}) custom-call(f32[128,512]{1,0:T(8,128)} %get-tuple-element.25.top_ref, f32[128,128]{1,0:T(8,128)} %get-tuple-element.26.inv_ref, f32[8,128]{1,0:T(8,128)} %get-tuple-element.27.log_ref, f32[128,768]{1,0:T(8,128)} %broadcast_select_fusion.4.rest_ref), custom_call_target="tpu_custom_call" | custom-call | tf_op jit(solution)/shard_map/other_panels/pallas_call | solution.py:172
  113.5 1.4 %bitcast_dynamic-update-slice_fusion.1 = f32[2,512,512]{2,1,0:T(8,128)S(1)} fusion(f32[2,512,512]{2,1,0:T(8,128)S(1)} %broadcast_in_dim.30, s32[]{:T(128)S(6)} %select_n.249, f32[512,512]{1,0:T(8,128)} %broadcast_select_fusion), kind=kLoop, calls=%fused_computation.2 | loop fusion | bytes 2097156 | tf_op jit(solution)/shard_map/dynamic_update_slice | solution.py:268
  115.9 1.3 %bitcast_dynamic-update-slice_fusion = f32[2,512,512]{2,1,0:T(8,128)S(1)} fusion(f32[2,512,512]{2,1,0:T(8,128)S(1)} %bitcast_dynamic-update-slice_fusion.1, s32[]{:T(128)S(6)} %select_n.251, f32[512,512]{1,0:T(8,128)} %collective-permute-done.14), kind=kLoop, calls=%fused_computation.1 | loop fusion | bytes 2097156 | tf_op jit(solution)/shard_map/dynamic_update_slice | solution.py:272
  117.3 1.9 %fusion.7 = f32[1024,512]{1,0:T(8,128)S(1)} fusion(f32[1024,512]{1,0:T(8,128)S(1)} %bitcast.12, f32[512,512]{1,0:T(8,128)S(1)} %copy-done.2), kind=kOutput, calls=%fused_computation.30 | convolution fusion | flops 1610612736 | bytes 5242880 | tf_op jit(solution)/shard_map/dot_general | solution.py:279
  119.1 2.0 %maximum_select_fusion = f32[512,1024]{0,1:T(8,128)S(1)} fusion(f32[512,512]{0,1:T(8,128)S(1)} %get-tuple-element.34, f32[512,1024]{0,1:T(8,128)S(1)} %copy-done.1, f32[512,512]{0,1:T(8,128)S(1)} %get-tuple-element.35, f32[1024,512]{1,0:T(8,128)S(1)} %fusion.7, pred[1024]{0:T(1024)(128)(4,1)S(1)} %fusion.3, pred[]{:T(512)S(6)} %gt.4), kind=kOutput, calls=%fused_computation | convolution fusion | flops 1612709888 | bytes 8389633 | tf_op jit(solution)/shard_map/dot_general | solution.py:280
  121.1 1.8 %copy.5 = f32[512,1024]{1,0:T(8,128)} copy(f32[512,1024]{0,1:T(8,128)S(1)} %maximum_select_fusion) | data formatting | bytes 4194304
  (42 shorter events, 11.5 us)
Async XLA Ops:
  0.6 10.3 %copy-start = (f32[512,1024]{1,0:T(8,128)S(1)}, f32[512,1024]{1,0:T(8,128)}, u32[]{:S(2)}) copy-start(f32[512,1024]{1,0:T(8,128)} %param.1) | copy-start | bytes 6291460
  1.8 9.2 %collective-permute-start = (f32[128,512]{1,0:T(8,128)S(1)}, f32[128,512]{1,0:T(8,128)S(1)}, u32[]{:S(2)}, u32[]{:S(2)}) collective-permute-start(f32[128,512]{1,0:T(8,128)S(1)} %slice.18), channel_id=1, source_target_pairs={{0,16}} | collective-permute-start | bytes 786440 | tf_op jit(solution)/shard_map/ppermute | solution.py:190
  5.3 17.2 %collective-permute-start.4 = (f32[512,512]{1,0:T(8,128)}, f32[512,512]{1,0:T(8,128)}, u32[]{:S(2)}, u32[]{:S(2)}) collective-permute-start(f32[512,512]{1,0:T(8,128)} %slice.22), channel_id=1, source_target_pairs={{0,2},{4,6},{8,10},{12,14},{16,18},{20,22},{24,26},{28,30}} | collective-permute-start | bytes 3145736 | tf_op jit(solution)/shard_map/ppermute | solution.py:190
  11.0 5.6 %collective-permute-start.1 = (f32[128,512]{1,0:T(8,128)S(1)}, f32[128,512]{1,0:T(8,128)}, u32[]{:S(2)}, u32[]{:S(2)}) collective-permute-start(f32[128,512]{1,0:T(8,128)S(1)} %broadcast_select_fusion.11), channel_id=1, source_target_pairs={{0,8},{16,24}} | collective-permute-start | bytes 786440 | tf_op jit(solution)/shard_map/ppermute | solution.py:190
  13.5 4.5 %collective-permute-start.3 = (f32[128,768]{1,0:T(8,128)S(1)}, f32[128,768]{1,0:T(8,128)}, u32[]{:S(2)}, u32[]{:S(2)}) collective-permute-start(f32[128,768]{1,0:T(8,128)S(1)} %pad_maximum_fusion), channel_id=1, source_target_pairs={{0,4}} | collective-permute-start | bytes 1179656 | tf_op jit(solution)/shard_map/ppermute | solution.py:190
  16.6 5.2 %collective-permute-start.2 = (f32[128,512]{1,0:T(8,128)S(1)}, f32[128,512]{1,0:T(8,128)S(1)}, u32[]{:S(2)}, u32[]{:S(2)}) collective-permute-start(f32[128,512]{1,0:T(8,128)S(1)} %broadcast_select_fusion.12), channel_id=1, source_target_pairs={{0,4},{16,20},{8,12},{24,28}} | collective-permute-start | bytes 786440 | tf_op jit(solution)/shard_map/ppermute | solution.py:190
  22.7 7.0 %copy-start.3 = (f32[512,512]{1,0:T(8,128)}, f32[512,512]{1,0:T(8,128)S(1)}, u32[]{:S(2)}) copy-start(f32[512,512]{1,0:T(8,128)S(1)} %broadcast_select_fusion.2) | copy-start | bytes 3145732
  22.7 7.0 %collective-permute-start.5 = (f32[512,512]{1,0:T(8,128)S(1)}, f32[512,512]{1,0:T(8,128)}, u32[]{:S(2)}, u32[]{:S(2)}) collective-permute-start(f32[512,512]{1,0:T(8,128)S(1)} %broadcast_select_fusion.2), channel_id=1, source_target_pairs={{0,1},{2,3},{4,5},{6,7},{8,9},{10,11},{12,13},{14,15},{16,17},{18,... | collective-permute-start | bytes 3145736 | tf_op jit(solution)/shard_map/ppermute | solution.py:190
  25.0 8.9 %copy-start.5 = (f32[128,512]{1,0:T(8,128)S(1)}, f32[128,512]{1,0:T(8,128)}, u32[]{:S(2)}) copy-start(f32[128,512]{1,0:T(8,128)} %broadcast_select_fusion.13) | copy-start | bytes 786436
  25.0 11.6 %collective-permute-start.8 = (f32[128,768]{1,0:T(8,128)S(1)}, f32[128,768]{1,0:T(8,128)S(1)}, u32[]{:S(2)}, u32[]{:S(2)}) collective-permute-start(f32[128,768]{1,0:T(8,128)S(1)} %broadcast_select_fusion.8), channel_id=1, source_target_pairs={{0,16},{4,20}} | collective-permute-start | bytes 1179656 | tf_op jit(solution)/shard_map/ppermute | solution.py:190
  26.4 7.5 %collective-permute-start.6 = (f32[128,512]{1,0:T(8,128)}, f32[128,512]{1,0:T(8,128)S(1)}, u32[]{:S(2)}, u32[]{:S(2)}) collective-permute-start(f32[128,512]{1,0:T(8,128)} %broadcast_select_fusion.13), channel_id=1, source_target_pairs={{0,2},{4,6},{8,10},{12,14},{16,18},{20,22},{24,26},{28,30}} | collective-permute-start | bytes 786440 | tf_op jit(solution)/shard_map/ppermute | solution.py:190
  31.2 16.4 %collective-permute-start.10 = (f32[512,512]{1,0:T(8,128)S(1)}, f32[512,512]{1,0:T(8,128)}, u32[]{:S(2)}, u32[]{:S(2)}) collective-permute-start(f32[512,512]{1,0:T(8,128)S(1)} %broadcast_select_fusion.3), channel_id=1, source_target_pairs={{0,8},{4,12},{9,17},{13,21},{18,26},{22,30},{27,3},{31,7}} | collective-permute-start | bytes 3145736 | tf_op jit(solution)/shard_map/ppermute | solution.py:242
  34.6 7.0 %collective-permute-start.7 = (f32[128,512]{1,0:T(8,128)}, f32[128,512]{1,0:T(8,128)}, u32[]{:S(2)}, u32[]{:S(2)}) collective-permute-start(f32[128,512]{1,0:T(8,128)} %broadcast_select_fusion.9), channel_id=1, source_target_pairs={{0,1},{4,5},{8,9},{12,13},{16,17},{20,21},{24,25},{28,29},{2,3},{6... | collective-permute-start | bytes 786440 | tf_op jit(solution)/shard_map/ppermute | solution.py:190
  37.4 9.1 %collective-permute-start.9 = (f32[128,768]{1,0:T(8,128)}, f32[128,768]{1,0:T(8,128)}, u32[]{:S(2)}, u32[]{:S(2)}) collective-permute-start(f32[128,768]{1,0:T(8,128)} %broadcast_select_fusion.6), channel_id=1, source_target_pairs={{0,8},{4,12},{16,24},{20,28}} | collective-permute-start | bytes 1179656 | tf_op jit(solution)/shard_map/ppermute | solution.py:190
  47.6 13.6 %copy-start.4 = (f32[128,768]{1,0:T(8,128)}, f32[128,768]{1,0:T(8,128)S(1)}, u32[]{:S(2)}) copy-start(f32[128,768]{1,0:T(8,128)S(1)} %broadcast_select_fusion.7) | copy-start | bytes 1179652
  48.8 31.1 %collective-permute-start.12 = (f32[512,512]{1,0:T(8,128)}, f32[512,512]{1,0:T(8,128)}, u32[]{:S(2)}, u32[]{:S(2)}) collective-permute-start(f32[512,512]{1,0:T(8,128)} %broadcast_select_fusion.1), channel_id=1, source_target_pairs={{0,24},{8,16},{4,28},{12,20},{9,1},{17,25},{13,5},{21,29},{18,10},... | collective-permute-start | bytes 3145736 | tf_op jit(solution)/shard_map/ppermute | solution.py:242
  50.1 11.1 %collective-permute-start.11 = (f32[128,768]{1,0:T(8,128)S(1)}, f32[128,768]{1,0:T(8,128)}, u32[]{:S(2)}, u32[]{:S(2)}) collective-permute-start(f32[128,768]{1,0:T(8,128)S(1)} %broadcast_select_fusion.7), channel_id=1, source_target_pairs={{0,2},{4,6},{16,18},{20,22},{8,10},{12,14},{24,26},{28,30}} | collective-permute-start | bytes 1179656 | tf_op jit(solution)/shard_map/ppermute | solution.py:190
  62.2 23.7 %collective-permute-start.13 = (f32[128,768]{1,0:T(8,128)S(1)}, f32[128,768]{1,0:T(8,128)}, u32[]{:S(2)}, u32[]{:S(2)}) collective-permute-start(f32[128,768]{1,0:T(8,128)S(1)} %broadcast_select_fusion.5), channel_id=1, source_target_pairs={{0,1},{4,5},{16,17},{20,21},{8,9},{12,13},{24,25},{28,29},{2,3},{6... | collective-permute-start | bytes 1179656 | tf_op jit(solution)/shard_map/ppermute | solution.py:190
  82.3 33.6 %collective-permute-start.14 = (f32[512,512]{1,0:T(8,128)}, f32[512,512]{1,0:T(8,128)}, u32[]{:S(2)}, u32[]{:S(2)}) collective-permute-start(f32[512,512]{1,0:T(8,128)} %broadcast_select_fusion), channel_id=1, source_target_pairs={{0,4},{4,0},{8,12},{12,8},{16,20},{20,16},{24,28},{28,24},{1,5},{5... | collective-permute-start | bytes 3145736 | tf_op jit(solution)/shard_map/ppermute | solution.py:271
  113.2 1.6 %copy-start.2 = (f32[512,512]{1,0:T(8,128)S(1)}, f32[512,512]{1,0:T(8,128)}, u32[]{:S(2)}) copy-start(f32[512,512]{1,0:T(8,128)} %get-tuple-element.29) | copy-start | bytes 3145732
  117.3 1.9 %copy-start.1 = (f32[512,1024]{0,1:T(8,128)S(1)}, f32[512,1024]{0,1:T(8,128)}, u32[]{:S(2)}) copy-start(f32[512,1024]{0,1:T(8,128)} %copy.3) | copy-start | bytes 6291460
